TPU v7x, 32 devices: a whole 2x2x4 slice. The times are simulated.
32 devices in a mesh: rad: 4 (over x, core), harm: 8 (over z, y).
Axes of the slice: x: 2, y: 2, z: 4, core: 2. Of those that a mesh axis runs over, the one named last changes fastest.
Arguments:
- velocity: bfloat16 [3, 16, 2, 256, 256], P(None, 'rad', None, 'harm'), may hold values from -6 to 6
- magnetic: bfloat16 [3, 16, 2, 256, 256], P(None, 'rad', None, 'harm'), may hold values from -6 to 6
- vorticity: bfloat16 [3, 16, 2, 256, 256], P(None, 'rad', None, 'harm'), may hold values from -6 to 6
- current: bfloat16 [3, 16, 2, 256, 256], P(None, 'rad', None, 'harm'), may hold values from -6 to 6
Outputs:
- advection: bfloat16 [3, 16, 2, 256, 256], P(None, 'rad', None, 'harm')
- induction_gradient: bfloat16 [3, 16, 2, 256, 256], P(None, 'rad', None, 'harm')
- energy_spectra: float32 [2, 16, 256], P(None, 'rad')
All inputs are finite; a program needn't handle non-finite values.
Results may differ from a plain program's by a relative error of at most 0.01.
Values may be sent and summed in bfloat16 or wider, within the bound.
A program may use at most 64 MiB of HBM per device.

v0:
```python
import functools

import jax
import jax.numpy as jnp
import numpy as np
from jax import lax
from jax.experimental import pallas as pl
from jax.experimental.pallas import tpu as pltpu
from jax.sharding import PartitionSpec as P

MESH = pl.DeviceIdType.MESH
PASSES = 2
BF = jnp.bfloat16
F32 = jnp.float32


def tables(degrees, thetas, points, harm_count):
    half = thetas // 2
    angles = np.pi * (np.arange(half) + 0.5) / thetas
    cosine = np.concatenate([np.cos(angles), -np.cos(angles)[::-1]])
    sine = np.concatenate([np.sin(angles), np.sin(angles)[::-1]])
    orders = np.arange(degrees)
    steps = np.arange(1, degrees)
    terms = 0.5 * np.log((2.0 * steps + 1.0) / (2.0 * steps))
    start = 0.5 * np.log(0.5) + np.concatenate([[0.0], np.cumsum(terms)])
    log_sector = start[:, None] + orders[:, None] * np.log(sine)[None, :]
    sectoral = np.exp(np.maximum(log_sector, -60.0)).astype(np.float32)
    unscale = np.exp(np.minimum(log_sector + 60.0, 0.0)).astype(np.float32)
    wave = np.arange(1, half + 1)
    series = np.cos(2.0 * wave[None, :] * angles[:, None]) / (4.0 * wave[None, :] ** 2 - 1.0)
    north = 2.0 / thetas * (1.0 - 2.0 * series.sum(axis=1))
    weights = np.concatenate([north, north[::-1]])
    weights = (weights * degrees / points).astype(np.float32)
    phase = 2.0 * np.pi * ((orders[:, None] * np.arange(points)[None, :]) % points) / points
    trig = np.stack([np.cos(phase), np.sin(phase)])
    trig = trig.reshape(2, harm_count, degrees // harm_count, points)
    trig = trig.transpose(1, 0, 2, 3).reshape(2 * degrees, points).astype(jnp.bfloat16)
    doubled = np.where(orders == 0, 1.0, 2.0).reshape(harm_count, 1, -1)
    doubled = np.broadcast_to(doubled, (harm_count, 2, degrees // harm_count)).reshape(-1, 1)
    analysis = (trig.astype(np.float32) * doubled).astype(jnp.bfloat16)
    return cosine.astype(np.float32), sectoral, unscale, weights, trig.T.copy(), analysis


def wide(column, width):
    return jnp.concatenate([column] * (width // column.shape[1]), axis=1)


def kernel(
    dims,
    cm_ref, x_ref, sect_ref, unscale_ref, w_ref, trig_ref, back_ref, energy_ref,
    out_ref, energy_out,
    tab, rows, outs, send, recv, grid, prod, send2, recv2, folded, spread, energy_all,
    ssem, rsem, ssem2, rsem2, esend, erecv,
):
    harm, shells, groups, modes, degrees, thetas, points, span = dims
    me = lax.axis_index("harm")
    pair_width = 2 * span
    block = min(16, modes)
    q_pairs = 6 // PASSES
    q_rows = 12 // PASSES * shells * 2

    barrier = pltpu.get_barrier_semaphore()
    for step in range(1, harm):
        peer = lax.rem(me + step, harm)
        pl.semaphore_signal(barrier, inc=1, device_id={"harm": peer}, device_id_type=MESH)

    order = (me * modes + lax.broadcasted_iota(jnp.int32, (modes, 128), 0)).astype(F32)
    order_square = order * order
    own = pl.ds(pl.multiple_of(me * modes, modes), modes)
    energy_all[me] = energy_ref[...]

    def table_block(step, carry):
        latest, before, inverse = carry
        for inner in range(16):
            degree = step * 16 + inner
            lf = jnp.full((modes, 128), degree, jnp.int32).astype(F32)
            dd = jnp.maximum(lf * lf - order_square, 1.0) / (4.0 * lf * lf - 1.0)
            guess = lax.rsqrt(dd)
            guess = guess * (1.5 - 0.5 * dd * guess * guess)
            live = lf > order
            alpha = jnp.where(live, guess, 0.0)
            starts = jnp.where(lf == order, 1.0, 0.0)
            new = wide(alpha, thetas) * (x_ref[...] * latest - wide(inverse, thetas) * before)
            new = new + wide(starts, thetas) * sect_ref[own, :]
            rows[inner] = new * unscale_ref[own, :]
            before, latest = latest, new
            inverse = jnp.where(live, dd * guess, 0.0)
        tab[:, pl.ds(pl.multiple_of(step * 16, 16), 16), :] = jnp.swapaxes(rows[...], 0, 1).astype(BF)
        return latest, before, inverse

    zero = jnp.zeros((modes, thetas), F32)
    lax.fori_loop(0, degrees // 16, table_block, (zero, zero, jnp.zeros((modes, 128), F32)))

    pl.semaphore_wait(barrier, harm - 1)

    def energy_copy(step):
        peer = lax.rem(me + step, harm)
        return pltpu.make_async_remote_copy(
            src_ref=energy_all.at[me], dst_ref=energy_all.at[me],
            send_sem=esend.at[step], recv_sem=erecv.at[step],
            device_id={"harm": peer}, device_id_type=MESH,
        )

    def forward(q, step):
        peer = lax.rem(me + step, harm)
        return pltpu.make_async_remote_copy(
            src_ref=send.at[peer, pl.ds(q * q_pairs, q_pairs)],
            dst_ref=recv.at[me, pl.ds(q * q_pairs, q_pairs)],
            send_sem=ssem.at[q, step], recv_sem=rsem.at[q, step],
            device_id={"harm": peer}, device_id_type=MESH,
        )

    def backward(pair, step):
        peer = lax.rem(me + step, harm)
        return pltpu.make_async_remote_copy(
            src_ref=send2.at[peer, pair], dst_ref=recv2.at[me, pair],
            send_sem=ssem2.at[pair, step], recv_sem=rsem2.at[pair, step],
            device_id={"harm": peer}, device_id_type=MESH,
        )

    for q in range(PASSES):
        def mode_block(mb, _, q=q):
            def one(i, _):
                m = mb * block + i
                outs[i] = jnp.dot(cm_ref[q, m], tab[m], preferred_element_type=F32) * (1.0 / degrees)
                return 0

            lax.fori_loop(0, block, one, 0, unroll=4)
            turned = jnp.swapaxes(outs[...], 0, 1)
            for s in range(shells):
                for pair in range(q_pairs):
                    for r in range(2):
                        k = (pair * 2 * shells + s) * 2 + r
                        first, second = turned[k], turned[k + 2 * shells]
                        for g in range(groups):
                            cut = slice(g * span, (g + 1) * span)
                            piece = jnp.concatenate([first[:, cut], second[:, cut]], axis=1).astype(BF)
                            at = pl.multiple_of(r * modes + mb * block, block)
                            send[s * groups + g, q * q_pairs + pair, pl.ds(at, block), :] = piece
            return 0

        lax.fori_loop(0, modes // block, mode_block, 0)
        for step in range(1, harm):
            forward(q, step).start()
        recv[me, pl.ds(q * q_pairs, q_pairs)] = send[me, pl.ds(q * q_pairs, q_pairs)]
    for step in range(1, harm):
        energy_copy(step).start()

    chunk = points // 3
    for q in range(PASSES):
        for step in range(1, harm):
            forward(q, step).wait_recv()
        for pair in range(q * q_pairs, (q + 1) * q_pairs):
            arrived = recv[:, pair].reshape(2 * degrees, pair_width)
            for part in range(3):
                cut = pl.ds(part * chunk, chunk)
                grid[pair, cut, :] = jnp.dot(trig_ref[cut, :], arrived, preferred_element_type=F32)

    piece_rows = 32

    def product_rows(i, _):
        at = pl.ds(pl.multiple_of(i * piece_rows, piece_rows), piece_rows)
        both = [grid[pair, at, :] for pair in range(6)]
        c = []
        for pair in range(6):
            c += [both[pair][:, :span], both[pair][:, span:]]
        u, b, w, j = c[0:3], c[3:6], c[6:9], c[9:12]

        def cross(a, d):
            return [a[1] * d[2] - a[2] * d[1], a[2] * d[0] - a[0] * d[2], a[0] * d[1] - a[1] * d[0]]

        lamb, lorentz, induced = cross(u, w), cross(j, b), cross(u, b)
        six = [lamb[n] + lorentz[n] for n in range(3)] + induced
        for pair in range(3):
            prod[pair, at, :] = jnp.concatenate([six[2 * pair], six[2 * pair + 1]], axis=1).astype(BF)
        return 0

    lax.fori_loop(0, points // piece_rows, product_rows, 0)

    per = 2 * modes
    for pair in range(3):
        analysed = jnp.dot(back_ref[...], prod[pair], preferred_element_type=F32)
        analysed = (analysed * w_ref[lax.rem(me, groups)]).astype(BF)
        send2[:, pair] = analysed.reshape(harm, per, pair_width)
        for step in range(1, harm):
            backward(pair, step).start()
        recv2[me, pair] = send2[me, pair]

    for pair in range(3):
        for step in range(1, harm):
            backward(pair, step).wait_recv()

        def fold_block(mb, _, pair=pair):
            for s in range(shells):
                for r in range(2):
                    at = pl.ds(pl.multiple_of(r * modes + mb * block, block), block)
                    got = [recv2[s * groups + g, pair, at, :].astype(F32) for g in range(groups)]
                    for c in range(2):
                        cut = slice(c * span, (c + 1) * span)
                        spread[(c * shells + s) * 2 + r] = jnp.concatenate([v[:, cut] for v in got], axis=1)
            here = pl.ds(pl.multiple_of(mb * block, block), block)
            folded[here, pl.ds(pair * 4 * shells, 4 * shells), :] = jnp.swapaxes(spread[...], 0, 1).astype(BF)
            return 0

        lax.fori_loop(0, modes // block, fold_block, 0)

    def spectrum(m, _):
        out_ref[m] = lax.dot_general(
            folded[m], tab[m], (((1,), (1,)), ((), ())), preferred_element_type=F32
        ).astype(BF)
        return 0

    lax.fori_loop(0, modes, spectrum, 0, unroll=4)

    for step in range(1, harm):
        energy_copy(step).wait_recv()
    energy_out[...] = jnp.sum(energy_all[...], axis=0)
    for step in range(1, harm):
        energy_copy(step).wait_send()
        for q in range(PASSES):
            forward(q, step).wait_send()
        for pair in range(3):
            backward(pair, step).wait_send()


def with_halo(block, axis):
    count = lax.axis_size(axis)
    up = [(i, i + 1) for i in range(count - 1)]
    down = [(b, a) for a, b in up]
    low = lax.ppermute(block[:, -1:], axis, up)
    high = lax.ppermute(block[:, :1], axis, down)
    return jnp.concatenate([low, block, high], axis=1)


def energy_weights(order_ints, degree_count):
    degrees = jnp.arange(degree_count, dtype=jnp.int32)
    order_col = order_ints[:, None]
    live_part = (degrees[None, :] >= order_col).astype(F32)
    inverse_modes = 1.0 / (2.0 * degrees.astype(F32) + 1.0)
    cosine_weight = jnp.where(order_col == 0, 0.5, 1.0)
    sine_weight = jnp.where(order_col == 0, 0.0, 1.0)
    scaled = live_part * inverse_modes[None, :]
    return jnp.stack([cosine_weight * scaled, sine_weight * scaled])


def local(velocity, magnetic, vorticity, current):
    harm = lax.axis_size("harm")
    me = lax.axis_index("harm")
    _, shells, _, modes, degrees = velocity.shape
    thetas, points = 3 * degrees // 2, 3 * degrees
    groups = harm // shells
    span = thetas // groups
    cosine, sectoral, unscale, weights, synthesis, analysis = tables(degrees, thetas, points, harm)

    own = me * modes + jnp.arange(modes, dtype=jnp.int32)
    energy_weight = energy_weights(own, degrees)
    energy = jnp.stack([
        jnp.sum(field.astype(F32) ** 2 * energy_weight[None, None], axis=(0, 2, 3))
        for field in (velocity, magnetic)
    ])

    fields = jnp.concatenate([velocity, magnetic, vorticity, current], axis=0)
    q_rows = 12 // PASSES * shells * 2
    cm = fields.reshape(PASSES, q_rows, modes, degrees).transpose(0, 2, 1, 3)
    x = jnp.asarray(np.broadcast_to(cosine[None, :], (modes, thetas)).copy())
    cut_weights = weights.reshape(groups, 1, span)
    w = jnp.asarray(np.concatenate([cut_weights, cut_weights], axis=2))

    block = min(16, modes)
    vmem = pl.BlockSpec(memory_space=pltpu.VMEM)
    dims = (harm, shells, groups, modes, degrees, thetas, points, span)
    spectra, total = pl.pallas_call(
        functools.partial(kernel, dims),
        name="dynamo",
        out_shape=(
            jax.ShapeDtypeStruct((modes, 12 * shells, degrees), BF),
            jax.ShapeDtypeStruct((2, shells, degrees), F32),
        ),
        in_specs=[vmem] * 8,
        out_specs=(vmem, vmem),
        scratch_shapes=[
            pltpu.VMEM((modes, degrees, thetas), BF),
            pltpu.VMEM((16, modes, thetas), F32),
            pltpu.VMEM((block, q_rows, thetas), F32),
            pltpu.VMEM((harm, 6, 2 * modes, 2 * span), BF),
            pltpu.VMEM((harm, 6, 2 * modes, 2 * span), BF),
            pltpu.VMEM((6, points, 2 * span), F32),
            pltpu.VMEM((3, points, 2 * span), BF),
            pltpu.VMEM((harm, 3, 2 * modes, 2 * span), BF),
            pltpu.VMEM((harm, 3, 2 * modes, 2 * span), BF),
            pltpu.VMEM((modes, 12 * shells, thetas), BF),
            pltpu.VMEM((4 * shells, block, thetas), F32),
            pltpu.VMEM((harm, 2, shells, degrees), F32),
            pltpu.SemaphoreType.DMA((PASSES, harm)),
            pltpu.SemaphoreType.DMA((PASSES, harm)),
            pltpu.SemaphoreType.DMA((3, harm)),
            pltpu.SemaphoreType.DMA((3, harm)),
            pltpu.SemaphoreType.DMA((harm,)),
            pltpu.SemaphoreType.DMA((harm,)),
        ],
        compiler_params=pltpu.CompilerParams(
            collective_id=0, has_side_effects=True, vmem_limit_bytes=60 * 1024 * 1024
        ),
    )(cm, x, jnp.asarray(sectoral), jnp.asarray(unscale), w, jnp.asarray(synthesis), jnp.asarray(analysis), energy)

    spectra = spectra.transpose(1, 0, 2).reshape(6, shells, 2, modes, degrees)
    rimmed = with_halo(spectra[3:], "rad").astype(F32)
    gradient = ((rimmed[:, 2:] - rimmed[:, :-2]) * 0.5).astype(BF)
    return spectra[:3], gradient, total


LANES = 128


def relay_tables(degrees, thetas, points, groups):
    half = thetas // 2
    rows = half // groups
    wide_rows = -(-rows // LANES) * LANES
    cosine, sectoral, unscale, weights, _, _ = tables(degrees, thetas, points, groups)

    def cut(array):
        parts = array[:, :half].reshape(-1, groups, rows).transpose(1, 0, 2)
        return np.pad(parts, ((0, 0), (0, 0), (0, wide_rows - rows)))

    x = cut(np.broadcast_to(cosine[None, :], (8, thetas)))
    w = np.tile(cut(np.broadcast_to(weights[None, :], (8, thetas))), (1, 1, 2))
    orders = np.arange(degrees)
    phase = 2.0 * np.pi * ((orders[:, None] * np.arange(points // 2)[None, :]) % points) / points
    trig = np.stack([np.cos(phase), np.sin(phase)]).astype(jnp.bfloat16).astype(np.float32)
    trig = trig.reshape(2, degrees // 2, 2, points // 2).transpose(2, 0, 1, 3)
    trig = trig.reshape(2, degrees, points // 2)
    doubled = np.where(orders == 0, 1.0, 2.0).reshape(degrees // 2, 2).T
    doubled = np.concatenate([doubled, doubled], axis=1)[:, :, None]
    synthesis = (trig.transpose(0, 2, 1) / degrees).astype(jnp.bfloat16)
    analysis = (trig * doubled).astype(jnp.bfloat16)
    return x, cut(sectoral), cut(unscale), w, synthesis, analysis


def cross(a, d):
    return [a[1] * d[2] - a[2] * d[1], a[2] * d[0] - a[0] * d[2], a[0] * d[1] - a[1] * d[0]]


def relay_kernel(
    dims,
    vel_ref, mag_ref, vor_ref, cur_ref, x_ref, sect_ref, unscale_ref, w_ref, trig_ref, back_ref, energy_ref,
    adv_ref, grad_ref, energy_out,
    tab, rows, rx, cs, outs, modes_buf, grid, prod, asc, souts, own, ysend, yrecv, zsend, land, halo, energy_all,
    lsem, zss, zrs, rss, rrs, yss, yrs, bss, brs, hss, hrs, esend, erecv,
):
    rads, harm, shells, groups, modes, degrees, thetas, points = dims
    me = lax.axis_index("harm")
    rad = lax.axis_index("rad")
    z, y = me // groups, me % groups
    other = 1 - y
    block = groups * modes
    top = degrees // 2
    fields = (vel_ref, mag_ref, vor_ref, cur_ref)
    low_half = [src * block < top for src in range(shells)]

    def at(zz, yy):
        return {"harm": zz * groups + yy}

    rad_up = {"rad": lax.rem(rad + 1, rads)}
    rad_down = {"rad": lax.rem(rad + rads - 1, rads)}

    barrier = pltpu.get_barrier_semaphore()
    for step in range(1, harm):
        pl.semaphore_signal(barrier, inc=1, device_id={"harm": lax.rem(me + step, harm)}, device_id_type=MESH)
    for target in (rad_up, rad_down):
        pl.semaphore_signal(barrier, inc=1, device_id=target, device_id_type=MESH)

    def lanes(low):
        return pl.ds(0, degrees) if low else pl.ds(top, degrees - top)

    def zcopy(f, dest, low, source):
        return pltpu.make_async_remote_copy(
            src_ref=fields[f].at[:, dest, :, :, lanes(low)],
            dst_ref=rx.at[source * groups + y, f, :, :, :, lanes(low)],
            send_sem=zss.at[dest, f], recv_sem=zrs.at[source, f],
            device_id=at(dest, y), device_id_type=MESH,
        )

    def relay_own(f, low):
        return pltpu.make_async_remote_copy(
            src_ref=fields[f].at[:, z, :, :, lanes(low)],
            dst_ref=rx.at[me, f, :, :, :, lanes(low)],
            send_sem=rss.at[z, f], recv_sem=rrs.at[z, f],
            device_id=at(z, other), device_id_type=MESH,
        )

    def relay(f, source, yy):
        slot = rx.at[source * groups + yy, f, :, :, :, lanes(low_half[source])]
        return pltpu.make_async_remote_copy(
            src_ref=slot, dst_ref=slot,
            send_sem=rss.at[source, f], recv_sem=rrs.at[source, f],
            device_id=at(z, other), device_id_type=MESH,
        )

    def local_copy(f):
        return pltpu.make_async_copy(fields[f].at[:, z], rx.at[me, f], lsem.at[f])

    for f in range(4):
        local_copy(f).start()
    energy_all[me] = energy_ref[...]
    pl.semaphore_wait(barrier, harm - 1 + 2)

    def dest_of(j):
        mark = shells - 1 - j
        return mark - jnp.where(mark <= z, 1, 0)

    for low in (True, False):
        @pl.when((z * block < top) == low)
        def _(low=low):
            for j in range(shells - 1):
                for f in range(4):
                    zcopy(f, dest_of(j), low, z).start()
            for f in range(4):
                relay_own(f, low).start()

    def energy_copy(step):
        peer = lax.rem(me + step, harm)
        return pltpu.make_async_remote_copy(
            src_ref=energy_all.at[me], dst_ref=energy_all.at[me],
            send_sem=esend.at[step], recv_sem=erecv.at[step],
            device_id={"harm": peer}, device_id_type=MESH,
        )

    for step in range(1, harm):
        energy_copy(step).start()

    def pass_on(source, f):
        zcopy(f, source, low_half[source], source).wait_recv()
        relay(f, source, y).start()

    early = z * (shells - 1 - z) == 0

    def pass_early(source, f):
        @pl.when(jnp.logical_and(early, z != source))
        def _():
            pass_on(source, f)

    def pass_late(source, f):
        @pl.when(jnp.logical_and(jnp.logical_not(early), z != source))
        def _():
            pass_on(source, f)

    x = x_ref[y, 0:1, :]
    width = x.shape[1]
    per = 16

    def table_block(source, starting, step, carry):
        first = source * block
        order = (first + lax.broadcasted_iota(jnp.int32, (block, width), 0)).astype(F32)
        square = order * order
        latest, before, inverse = carry
        for inner in range(per):
            degree = step * per + inner
            lf = jnp.full((1, width), degree, jnp.int32).astype(F32)
            scale = 1.0 / (4.0 * lf * lf - 1.0)
            gap = lf * lf - square
            if starting:
                gap = jnp.maximum(gap, 1.0)
            dd = gap * scale
            guess = lax.rsqrt(dd)
            guess = guess * (1.5 - 0.5 * dd * guess * guess)
            root = dd * guess
            if starting:
                live = lf > order
                guess = jnp.where(live, guess, 0.0)
                root = jnp.where(live, root, 0.0)
            new = guess * (x * latest - inverse * before)
            if starting:
                new = new + jnp.where(lf == order, sect_ref[y, pl.ds(first, block), :], 0.0)
            rows[inner] = new * unscale_ref[y, pl.ds(first, block), :]
            before, latest = latest, new
            inverse = root
        here = pl.ds(pl.multiple_of(step * per, per), per)
        tab[pl.ds(first, block), here, :] = jnp.swapaxes(rows[...], 0, 1).astype(BF)
        return latest, before, inverse

    def table_start(source):
        first = source * block
        floor = 0 if low_half[source] else top
        if first > floor:
            tab[pl.ds(first, block), pl.ds(floor, first - floor), :] = jnp.zeros((block, first - floor, width), BF)
        zero = jnp.zeros((block, width), F32)
        return lax.fori_loop(
            first // per, (first + block) // per, functools.partial(table_block, source, True), (zero, zero, zero))

    def table_rest(source, carry, low, high):
        return lax.fori_loop(low, high, functools.partial(table_block, source, False), carry)

    steps = degrees // per
    for source in reversed(range(shells)):
        first = (source + 1) * block // per
        carry = table_start(source)
        if low_half[source]:
            count = 4
            edges = [first + (steps - first) * i // count for i in range(count + 1)]
            for f in range(count):
                carry = table_rest(source, carry, edges[f], edges[f + 1])
                pass_early(source, f)
        else:
            table_rest(source, carry, first, steps)
            for f in range(4):
                @pl.when(z != source)
                def _(f=f):
                    pass_on(source, f)
    for f in range(4):
        for source in reversed(range(shells)):
            if low_half[source]:
                pass_late(source, f)

    lane = lax.broadcasted_iota(jnp.int32, (24, degrees), 1) % 2
    half_modes = modes // 2

    def transform(b, low):
        cut = slice(0, degrees) if low else slice(top, degrees)
        cs[:, :, cut] = jnp.swapaxes(
            rx[b].reshape(24, modes, degrees)[:, :, cut].astype(F32), 0, 1)
        for par in range(2):
            for i in range(half_modes):
                c = cs[2 * i + par, :, cut]
                even = lane[:, cut] == par
                left = jnp.concatenate([jnp.where(even, c, 0.0), jnp.where(even, 0.0, c)], axis=0).astype(BF)
                m = b * modes + 2 * i + par
                eo = jnp.dot(left, tab[m, cut, :], preferred_element_type=F32)
                outs[i] = jnp.concatenate([eo[:24] + eo[24:], eo[:24] - eo[24:]], axis=1)
            turned = jnp.swapaxes(outs[...], 0, 1).astype(BF)
            for k in range(24):
                c, r = k // 2, k % 2
                here = pl.ds(pl.multiple_of(r * top + b * half_modes, half_modes), half_modes)
                modes_buf[par, c, here, :] = turned[k]

    for f in range(4):
        local_copy(f).wait()
    for source in reversed(range(shells)):
        for f in range(4):
            relay(f, source, other).wait_recv()

        def both(yy, _, source=source):
            transform(source * groups + yy, low_half[source])
            return 0

        lax.fori_loop(0, groups, both, 0)

    def synth(c, _):
        for par in range(2):
            grid[par, c] = jnp.dot(trig_ref[par], modes_buf[par, c], preferred_element_type=F32)
        return 0

    lax.fori_loop(0, 12, synth, 0)

    piece = 16

    def product_rows(i, _):
        at_rows = pl.ds(pl.multiple_of((i // 2) * piece, piece), piece)
        at_lanes = pl.ds(pl.multiple_of((i % 2) * width, width), width)
        e = [grid[0, c, at_rows, at_lanes] for c in range(12)]
        o = [grid[1, c, at_rows, at_lanes] for c in range(12)]
        sides = []
        for g in ([a + d for a, d in zip(e, o)], [a - d for a, d in zip(e, o)]):
            u, b, w, j = g[0:3], g[3:6], g[6:9], g[9:12]
            lamb, lorentz, induced = cross(u, w), cross(j, b), cross(u, b)
            sides.append([lamb[n] + lorentz[n] for n in range(3)] + induced)
        for c in range(6):
            prod[0, c, at_rows, at_lanes] = (sides[0][c] + sides[1][c]).astype(BF)
            prod[1, c, at_rows, at_lanes] = (sides[0][c] - sides[1][c]).astype(BF)
        return 0

    lax.fori_loop(0, points // 2 // piece * 2, product_rows, 0)

    def analyse(c, _):
        for par in range(2):
            a = jnp.dot(back_ref[par], prod[par, c], preferred_element_type=F32)
            a = a * w_ref[y, 0:1, :]
            plus, minus = a[:, :width] + a[:, width:], a[:, :width] - a[:, width:]
            for r in range(2):
                cut = slice(r * top, (r + 1) * top)
                asc[par, 2 * c + r] = plus[cut]
                asc[par, 16 + 2 * c + r] = minus[cut]
        return 0

    lax.fori_loop(0, 6, analyse, 0)

    out_lane = lax.broadcasted_iota(jnp.int32, (16, degrees), 1) % 2

    def spectrum(b, low):
        cut = slice(0, degrees) if low else slice(top, degrees)
        for par in range(2):
            here = pl.ds(pl.multiple_of(b * half_modes, half_modes), half_modes)
            turned = jnp.swapaxes(asc[par, :, here, :], 0, 1).astype(BF)
            for i in range(half_modes):
                m = b * modes + 2 * i + par
                both = lax.dot_general(
                    turned[i], tab[m, cut, :], (((1,), (1,)), ((), ())), preferred_element_type=F32)
                souts[2 * i + par, :, cut] = jnp.where(out_lane[:, cut] == par, both[:16], both[16:])
        return jnp.swapaxes(souts[:, :, cut], 0, 1)[:12]

    def ycopy(target):
        low = low_half[target]
        return pltpu.make_async_remote_copy(
            src_ref=ysend.at[target, :, :, lanes(low)], dst_ref=yrecv.at[target, :, :, lanes(low)],
            send_sem=yss.at[target], recv_sem=yrs.at[target],
            device_id=at(z, other), device_id_type=MESH,
        )

    def bcopy(target, shell, low):
        return pltpu.make_async_remote_copy(
            src_ref=zsend.at[target, :, :, lanes(low)], dst_ref=land.at[shell, :, :, lanes(low)],
            send_sem=bss.at[target], recv_sem=brs.at[shell],
            device_id=at(target, y), device_id_type=MESH,
        )

    @pl.when(z * block >= top)
    def _():
        land[:, :, :, 0:top] = jnp.zeros((shells, 12, modes, top), BF)

    for target in range(shells):
        low = low_half[target]
        cut = slice(0, degrees) if low else slice(top, degrees)
        ysend[target, :, :, cut] = spectrum(target * groups + other, low).astype(BF)
        ycopy(target).start()
        own[target, :, :, cut] = spectrum(target * groups + y, low)

    for target in range(shells):
        low = low_half[target]
        cut = slice(0, degrees) if low else slice(top, degrees)
        ycopy(target).wait_recv()
        total = (own[target, :, :, cut] + yrecv[target, :, :, cut].astype(F32)).astype(BF)

        @pl.when(z == target)
        def _():
            land[target, :, :, cut] = total

        @pl.when(z != target)
        def _():
            zsend[target, :, :, cut] = total
            bcopy(target, z, low).start()

    def arrived(shell):
        for low in (True, False):
            @pl.when(jnp.logical_and(z != shell, (z * block < top) == low))
            def _(low=low):
                bcopy(shell, shell, low).wait_recv()

    def hcopy(side):
        shell = shells - 1 if side == 0 else 0
        return pltpu.make_async_remote_copy(
            src_ref=land.at[shell, pl.ds(6, 6)], dst_ref=halo.at[side],
            send_sem=hss.at[side], recv_sem=hrs.at[side],
            device_id=rad_up if side == 0 else rad_down, device_id_type=MESH,
        )

    arrived(shells - 1)
    hcopy(0).start()
    arrived(0)
    hcopy(1).start()
    for shell in range(1, shells - 1):
        arrived(shell)
    for step in range(1, harm):
        energy_copy(step).wait_recv()
    energy_out[...] = jnp.sum(energy_all[...], axis=0)
    for shell in range(shells):
        for k in range(6):
            adv_ref[k // 2, shell, k % 2] = land[shell, k]
    hcopy(0).wait_recv()
    hcopy(1).wait_recv()
    for shell in range(shells):
        for k in range(6):
            if shell > 0:
                before = land[shell - 1, 6 + k].astype(F32)
            else:
                before = jnp.where(rad > 0, halo[0, k].astype(F32), 0.0)
            if shell < shells - 1:
                after = land[shell + 1, 6 + k].astype(F32)
            else:
                after = jnp.where(rad < rads - 1, halo[1, k].astype(F32), 0.0)
            grad_ref[k // 2, shell, k % 2] = ((after - before) * 0.5).astype(BF)

    hcopy(0).wait_send()
    hcopy(1).wait_send()
    for step in range(1, harm):
        energy_copy(step).wait_send()
    for low in (True, False):
        @pl.when((z * block < top) == low)
        def _(low=low):
            for j in range(shells - 1):
                for f in range(4):
                    zcopy(f, dest_of(j), low, z).wait_send()
    for source in range(shells):
        for f in range(4):
            relay(f, source, y).wait_send()
        ycopy(source).wait_send()

        @pl.when(z != source)
        def _(source=source):
            bcopy(source, z, low_half[source]).wait_send()


def energy_parts(velocity, magnetic, own, degrees):
    energy_weight = energy_weights(own, degrees)
    return jnp.stack([
        jnp.sum(field.astype(F32) ** 2 * energy_weight[None, None], axis=(0, 2, 3))
        for field in (velocity, magnetic)
    ])


def local_relay(velocity, magnetic, vorticity, current):
    harm, rads = lax.axis_size("harm"), lax.axis_size("rad")
    me = lax.axis_index("harm")
    _, shells, _, modes, degrees = velocity.shape
    thetas, points = 3 * degrees // 2, 3 * degrees
    groups = harm // shells
    x, sect, unscale, w, synthesis, analysis = relay_tables(degrees, thetas, points, groups)
    width = x.shape[2]
    block = groups * modes
    own = me * modes + jnp.arange(modes, dtype=jnp.int32)
    energy = energy_parts(velocity, magnetic, own, degrees)
    vmem = pl.BlockSpec(memory_space=pltpu.VMEM)
    hbm = pl.BlockSpec(memory_space=pl.ANY)
    dims = (rads, harm, shells, groups, modes, degrees, thetas, points)
    result = jax.ShapeDtypeStruct(velocity.shape, BF)
    dma = pltpu.SemaphoreType.DMA
    return pl.pallas_call(
        functools.partial(relay_kernel, dims),
        name="dynamo",
        out_shape=(result, result, jax.ShapeDtypeStruct((2, shells, degrees), F32)),
        in_specs=[hbm] * 4 + [vmem] * 7,
        out_specs=(vmem, vmem, vmem),
        scratch_shapes=[
            pltpu.VMEM((degrees, degrees, width), BF),
            pltpu.VMEM((16, block, width), F32),
            pltpu.VMEM((harm, 4, 3, 2, modes, degrees), BF),
            pltpu.VMEM((modes, 24, degrees), F32),
            pltpu.VMEM((modes // 2, 24, 2 * width), F32),
            pltpu.VMEM((2, 12, degrees, 2 * width), BF),
            pltpu.VMEM((2, 12, points // 2, 2 * width), F32),
            pltpu.VMEM((2, 6, points // 2, 2 * width), BF),
            pltpu.VMEM((2, 32, degrees // 2, width), F32),
            pltpu.VMEM((modes, 16, degrees), F32),
            pltpu.VMEM((shells, 12, modes, degrees), F32),
            pltpu.VMEM((shells, 12, modes, degrees), BF),
            pltpu.VMEM((shells, 12, modes, degrees), BF),
            pltpu.VMEM((shells, 12, modes, degrees), BF),
            pltpu.VMEM((shells, 12, modes, degrees), BF),
            pltpu.VMEM((2, 6, modes, degrees), BF),
            pltpu.VMEM((harm, 2, shells, degrees), F32),
            dma((4,)), dma((shells, 4)), dma((shells, 4)), dma((shells, 4)), dma((shells, 4)),
            dma((shells,)), dma((shells,)), dma((shells,)), dma((shells,)),
            dma((2,)), dma((2,)), dma((harm,)), dma((harm,)),
        ],
        compiler_params=pltpu.CompilerParams(
            collective_id=0, has_side_effects=True, vmem_limit_bytes=62 * 1024 * 1024
        ),
    )(velocity, magnetic, vorticity, current, jnp.asarray(x), jnp.asarray(sect), jnp.asarray(unscale),
      jnp.asarray(w), jnp.asarray(synthesis), jnp.asarray(analysis), energy)


def relay_fits(mesh, args):
    _, total, _, degrees, _ = args[0].shape
    rads, harm = mesh.shape["rad"], mesh.shape["harm"]
    shells, modes = total // rads, degrees // harm
    return harm == 2 * shells and rads > 2 and modes % 32 == 0 and degrees % (2 * LANES) == 0


def solution(mesh):
    spec = P(None, "rad", None, "harm", None)

    def run(*args):
        body = local_relay if relay_fits(mesh, args) else local
        return jax.shard_map(
            body,
            mesh=mesh,
            in_specs=(spec,) * 4,
            out_specs=(spec, spec, P(None, "rad", None)),
            check_vma=False,
        )(*args)

    return run
```

profile of v0, /device:TPU:8, one launch (start us, length us, event | category | flops | bytes accessed | tf_op | source)
XLA Modules:
  0.0 86.0 jit_solution(15666540302205076576)
XLA Ops:
  0.7 0.1 select_multiply_fusion.1
  0.8 1.3 %multiply_reduce_fusion.1 = (f32[4,256]{1,0:T(4,128)S(1)}, f32[4,256]{1,0:T(4,128)S(1)}) fusion(bf16[3,4,2,32,256]{4,3,2,1,0:T(8,128)(2,1)} %vel_ref.1, f32[2,32,256]{2,1,0:T(8,128)S(1)} %pad_maximum_fusion, bf16[3,4,2,32,256]{4,3,2,1,0:T(8,128)(2,1)} %mag_ref.1), kind=kLoop, calls=%fused_computation.1 | loop fusion | flops 1570816 | bytes 860160 | tf_op jit(solution)/shard_map/reduce_sum | solution.py:704
  2.1 0.6 pad_maximum_fusion.1.energy_ref
  2.7 80.1 %dynamo.1 = (bf16[3,4,2,32,256]{4,3,2,1,0:T(8,128)(2,1)}, bf16[3,4,2,32,256]{4,3,2,1,0:T(8,128)(2,1)}, f32[2,4,256]{2,1,0:T(4,128)}) custom-call(bf16[3,4,2,32,256]{4,3,2,1,0:T(8,128)(2,1)} %vel_ref.1, bf16[3,4,2,32,256]{4,3,2,1,0:T(8,128)(2,1)} %mag_ref.1, bf16[3,4,2,32,256]{4,3,2,1,0:T(8,128)(2,1)} %vor_ref.1, bf16[3,4,2,32,256]{4,3,2,1,0:T(8,128)(2,1)} %cur_ref.1, ...), custom_call_target="tpu_custom_call" | custom-call | tf_op jit(solution)/shard_map/dynamo/pallas_call | solution.py:725
  82.8 0.0 copy-start
  82.8 1.8 %copy.16 = bf16[3,4,2,32,256]{4,3,2,1,0:T(8,128)(2,1)} copy(bf16[3,4,2,32,256]{4,3,2,1,0:T(8,128)(2,1)} %get-tuple-element.12) | data formatting | bytes 786432
  84.6 0.0 copy-done
  84.6 0.0 copy-start.1
  84.6 0.7 copy.17
  85.4 0.0 copy-done.1
  85.4 0.6 copy.18
  (4 shorter events, 0.0 us)
Async XLA Ops:
  82.8 1.8 %copy-start = (bf16[3,4,2,32,256]{4,3,2,1,0:T(8,128)(2,1)S(1)}, bf16[3,4,2,32,256]{4,3,2,1,0:T(8,128)(2,1)}, u32[]{:S(2)}) copy-start(bf16[3,4,2,32,256]{4,3,2,1,0:T(8,128)(2,1)} %get-tuple-element.13) | copy-start | bytes 1179652
  84.6 0.8 copy-start.1
where the time goes:
time: 86.2 us; the launch traced here: 86 us
  Pallas kernels  80.1 us (93%)
  local copies, waits for them, and re-layouts  3.17 us (4%)
  other arithmetic  2.05 us (2%)
    pallas_call x1, Pallas kernels, local_relay(): pl.pallas_call(functools.partial(relay_kernel, dims), name='dynamo', out_...  80.1 us
    unnamed x7, local copies, waits for them, and re-layouts  3.17 us

commit v1 on v0

--- a/solution.py
+++ b/solution.py
@@ -342,23 +342,27 @@
 
 def relay_kernel(
     dims,
-    vel_ref, mag_ref, vor_ref, cur_ref, x_ref, sect_ref, unscale_ref, w_ref, trig_ref, back_ref, energy_ref,
+    vel_ref, mag_ref, vor_ref, cur_ref, x_ref, sect_ref, unscale_ref, w_ref, trig_ref, back_ref,
     adv_ref, grad_ref, energy_out,
-    tab, rows, rx, cs, outs, modes_buf, grid, prod, asc, souts, own, ysend, yrecv, zsend, land, halo, energy_all,
-    lsem, zss, zrs, rss, rrs, yss, yrs, bss, brs, hss, hrs, esend, erecv,
+    tab, rows, rx, cs, outs, modes_buf, grid, prod, asc, souts, own, ysend, yrecv, zsend, land, halo, energy_all, held,
+    lsem, vsem, zss, zrs, rss, rrs, yss, yrs, bss, brs, hss, hrs, esend, erecv,
 ):
     rads, harm, shells, groups, modes, degrees, thetas, points = dims
     me = lax.axis_index("harm")
     rad = lax.axis_index("rad")
     z, y = me // groups, me % groups
-    other = 1 - y
+    base, core = rad // groups * groups, rad % groups
+    other = 1 - core
+    straight = core == y
     block = groups * modes
     top = degrees // 2
     fields = (vel_ref, mag_ref, vor_ref, cur_ref)
     low_half = [src * block < top for src in range(shells)]
 
-    def at(zz, yy):
-        return {"harm": zz * groups + yy}
+    def mate(shell):
+        return {"rad": base + y, "harm": shell * groups + core}
+
+    partner = {"rad": base + other}
 
     rad_up = {"rad": lax.rem(rad + 1, rads)}
     rad_down = {"rad": lax.rem(rad + rads - 1, rads)}
@@ -369,23 +373,20 @@
     for target in (rad_up, rad_down):
         pl.semaphore_signal(barrier, inc=1, device_id=target, device_id_type=MESH)
 
+    @pl.when(jnp.logical_not(straight))
+    def _():
+        for shell in range(shells):
+            pl.semaphore_signal(barrier, inc=1, device_id=mate(shell), device_id_type=MESH)
+
     def lanes(low):
         return pl.ds(0, degrees) if low else pl.ds(top, degrees - top)
 
     def zcopy(f, dest, low, source):
         return pltpu.make_async_remote_copy(
             src_ref=fields[f].at[:, dest, :, :, lanes(low)],
-            dst_ref=rx.at[source * groups + y, f, :, :, :, lanes(low)],
+            dst_ref=rx.at[me, f, :, :, :, lanes(low)],
             send_sem=zss.at[dest, f], recv_sem=zrs.at[source, f],
-            device_id=at(dest, y), device_id_type=MESH,
-        )
-
-    def relay_own(f, low):
-        return pltpu.make_async_remote_copy(
-            src_ref=fields[f].at[:, z, :, :, lanes(low)],
-            dst_ref=rx.at[me, f, :, :, :, lanes(low)],
-            send_sem=rss.at[z, f], recv_sem=rrs.at[z, f],
-            device_id=at(z, other), device_id_type=MESH,
+            device_id=mate(dest), device_id_type=MESH,
         )
 
     def relay(f, source, yy):
@@ -393,16 +394,24 @@
         return pltpu.make_async_remote_copy(
             src_ref=slot, dst_ref=slot,
             send_sem=rss.at[source, f], recv_sem=rrs.at[source, f],
-            device_id=at(z, other), device_id_type=MESH,
+            device_id=partner, device_id_type=MESH,
         )
 
     def local_copy(f):
         return pltpu.make_async_copy(fields[f].at[:, z], rx.at[me, f], lsem.at[f])
 
-    for f in range(4):
-        local_copy(f).start()
-    energy_all[me] = energy_ref[...]
-    pl.semaphore_wait(barrier, harm - 1 + 2)
+    def held_copy(f):
+        return pltpu.make_async_copy(fields[f], held.at[f], vsem.at[f])
+
+    for f in range(2):
+        held_copy(f).start()
+
+    @pl.when(straight)
+    def _():
+        for f in range(4):
+            local_copy(f).start()
+
+    pl.semaphore_wait(barrier, harm - 1 + 2 + shells * jnp.where(straight, 0, 1))
 
     def dest_of(j):
         mark = shells - 1 - j
@@ -414,8 +423,11 @@
             for j in range(shells - 1):
                 for f in range(4):
                     zcopy(f, dest_of(j), low, z).start()
-            for f in range(4):
-                relay_own(f, low).start()
+
+            @pl.when(jnp.logical_not(straight))
+            def _():
+                for f in range(4):
+                    zcopy(f, z, low, z).start()
 
     def energy_copy(step):
         peer = lax.rem(me + step, harm)
@@ -425,26 +437,19 @@
             device_id={"harm": peer}, device_id_type=MESH,
         )
 
-    for step in range(1, harm):
-        energy_copy(step).start()
-
-    def pass_on(source, f):
-        zcopy(f, source, low_half[source], source).wait_recv()
-        relay(f, source, y).start()
-
-    early = z * (shells - 1 - z) == 0
-
-    def pass_early(source, f):
-        @pl.when(jnp.logical_and(early, z != source))
-        def _():
-            pass_on(source, f)
-
-    def pass_late(source, f):
-        @pl.when(jnp.logical_and(jnp.logical_not(early), z != source))
-        def _():
-            pass_on(source, f)
-
-    x = x_ref[y, 0:1, :]
+    def pass_on(source):
+        for f in range(4):
+            @pl.when(jnp.logical_and(straight, z == source))
+            def _(f=f):
+                local_copy(f).wait()
+
+            @pl.when(jnp.logical_not(jnp.logical_and(straight, z == source)))
+            def _(f=f):
+                zcopy(f, source, low_half[source], source).wait_recv()
+
+            relay(f, source, core).start()
+
+    x = x_ref[core, 0:1, :]
     width = x.shape[1]
     per = 16
 
@@ -470,8 +475,8 @@
                 root = jnp.where(live, root, 0.0)
             new = guess * (x * latest - inverse * before)
             if starting:
-                new = new + jnp.where(lf == order, sect_ref[y, pl.ds(first, block), :], 0.0)
-            rows[inner] = new * unscale_ref[y, pl.ds(first, block), :]
+                new = new + jnp.where(lf == order, sect_ref[core, pl.ds(first, block), :], 0.0)
+            rows[inner] = new * unscale_ref[core, pl.ds(first, block), :]
             before, latest = latest, new
             inverse = root
         here = pl.ds(pl.multiple_of(step * per, per), per)
@@ -492,24 +497,31 @@
 
     steps = degrees // per
     for source in reversed(range(shells)):
-        first = (source + 1) * block // per
         carry = table_start(source)
-        if low_half[source]:
-            count = 4
-            edges = [first + (steps - first) * i // count for i in range(count + 1)]
-            for f in range(count):
-                carry = table_rest(source, carry, edges[f], edges[f + 1])
-                pass_early(source, f)
-        else:
-            table_rest(source, carry, first, steps)
-            for f in range(4):
-                @pl.when(z != source)
-                def _(f=f):
-                    pass_on(source, f)
-    for f in range(4):
-        for source in reversed(range(shells)):
-            if low_half[source]:
-                pass_late(source, f)
+        lax.fori_loop((source + 1) * block // per, steps, functools.partial(table_block, source, False), carry)
+
+    for f in range(2):
+        held_copy(f).wait()
+    own_order = me * modes + lax.broadcasted_iota(jnp.int32, (modes, degrees), 0)
+    degree = lax.broadcasted_iota(jnp.int32, (modes, degrees), 1)
+    share = jnp.where(degree >= own_order, 1.0 / (2.0 * degree.astype(F32) + 1.0), 0.0)
+    parts = (share * jnp.where(own_order == 0, 0.5, 1.0), share * jnp.where(own_order == 0, 0.0, 1.0))
+
+    def shell_energy(shell, _):
+        for f in range(2):
+            total = jnp.zeros((modes, degrees), F32)
+            for r in range(2):
+                square = jnp.zeros((modes, degrees), F32)
+                for c in range(3):
+                    value = held[f, c, shell, r].astype(F32)
+                    square = square + value * value
+                total = total + square * parts[r]
+            energy_all[me, f, pl.ds(shell, 1), :] = jnp.sum(total, axis=0, keepdims=True)
+        return 0
+
+    lax.fori_loop(0, shells, shell_energy, 0)
+    for step in range(1, harm):
+        energy_copy(step).start()
 
     lane = lax.broadcasted_iota(jnp.int32, (24, degrees), 1) % 2
     half_modes = modes // 2
@@ -532,17 +544,17 @@
                 here = pl.ds(pl.multiple_of(r * top + b * half_modes, half_modes), half_modes)
                 modes_buf[par, c, here, :] = turned[k]
 
-    for f in range(4):
-        local_copy(f).wait()
-    for source in reversed(range(shells)):
+    def partner_block(source):
         for f in range(4):
             relay(f, source, other).wait_recv()
-
-        def both(yy, _, source=source):
-            transform(source * groups + yy, low_half[source])
-            return 0
-
-        lax.fori_loop(0, groups, both, 0)
+        transform(source * groups + other, low_half[source])
+
+    for source in reversed(range(shells)):
+        pass_on(source)
+        if source + 1 < shells:
+            partner_block(source + 1)
+        transform(source * groups + core, low_half[source])
+    partner_block(0)
 
     def synth(c, _):
         for par in range(2):
@@ -573,7 +585,7 @@
     def analyse(c, _):
         for par in range(2):
             a = jnp.dot(back_ref[par], prod[par, c], preferred_element_type=F32)
-            a = a * w_ref[y, 0:1, :]
+            a = a * w_ref[core, 0:1, :]
             plus, minus = a[:, :width] + a[:, width:], a[:, :width] - a[:, width:]
             for r in range(2):
                 cut = slice(r * top, (r + 1) * top)
@@ -602,14 +614,14 @@
         return pltpu.make_async_remote_copy(
             src_ref=ysend.at[target, :, :, lanes(low)], dst_ref=yrecv.at[target, :, :, lanes(low)],
             send_sem=yss.at[target], recv_sem=yrs.at[target],
-            device_id=at(z, other), device_id_type=MESH,
+            device_id=partner, device_id_type=MESH,
         )
 
     def bcopy(target, shell, low):
         return pltpu.make_async_remote_copy(
             src_ref=zsend.at[target, :, :, lanes(low)], dst_ref=land.at[shell, :, :, lanes(low)],
             send_sem=bss.at[target], recv_sem=brs.at[shell],
-            device_id=at(target, y), device_id_type=MESH,
+            device_id=mate(target), device_id_type=MESH,
         )
 
     @pl.when(z * block >= top)
@@ -621,7 +633,7 @@
         cut = slice(0, degrees) if low else slice(top, degrees)
         ysend[target, :, :, cut] = spectrum(target * groups + other, low).astype(BF)
         ycopy(target).start()
-        own[target, :, :, cut] = spectrum(target * groups + y, low)
+        own[target, :, :, cut] = spectrum(target * groups + core, low)
 
     for target in range(shells):
         low = low_half[target]
@@ -629,18 +641,20 @@
         ycopy(target).wait_recv()
         total = (own[target, :, :, cut] + yrecv[target, :, :, cut].astype(F32)).astype(BF)
 
-        @pl.when(z == target)
+        stays = jnp.logical_and(straight, z == target)
+
+        @pl.when(stays)
         def _():
             land[target, :, :, cut] = total
 
-        @pl.when(z != target)
+        @pl.when(jnp.logical_not(stays))
         def _():
             zsend[target, :, :, cut] = total
             bcopy(target, z, low).start()
 
     def arrived(shell):
         for low in (True, False):
-            @pl.when(jnp.logical_and(z != shell, (z * block < top) == low))
+            @pl.when(jnp.logical_and(jnp.logical_not(jnp.logical_and(straight, z == shell)), (z * block < top) == low))
             def _(low=low):
                 bcopy(shell, shell, low).wait_recv()
 
@@ -688,35 +702,30 @@
             for j in range(shells - 1):
                 for f in range(4):
                     zcopy(f, dest_of(j), low, z).wait_send()
+
+            @pl.when(jnp.logical_not(straight))
+            def _():
+                for f in range(4):
+                    zcopy(f, z, low, z).wait_send()
+
     for source in range(shells):
         for f in range(4):
-            relay(f, source, y).wait_send()
+            relay(f, source, core).wait_send()
         ycopy(source).wait_send()
 
-        @pl.when(z != source)
+        @pl.when(jnp.logical_not(jnp.logical_and(straight, z == source)))
         def _(source=source):
             bcopy(source, z, low_half[source]).wait_send()
 
 
-def energy_parts(velocity, magnetic, own, degrees):
-    energy_weight = energy_weights(own, degrees)
-    return jnp.stack([
-        jnp.sum(field.astype(F32) ** 2 * energy_weight[None, None], axis=(0, 2, 3))
-        for field in (velocity, magnetic)
-    ])
-
-
 def local_relay(velocity, magnetic, vorticity, current):
     harm, rads = lax.axis_size("harm"), lax.axis_size("rad")
-    me = lax.axis_index("harm")
     _, shells, _, modes, degrees = velocity.shape
     thetas, points = 3 * degrees // 2, 3 * degrees
     groups = harm // shells
     x, sect, unscale, w, synthesis, analysis = relay_tables(degrees, thetas, points, groups)
     width = x.shape[2]
     block = groups * modes
-    own = me * modes + jnp.arange(modes, dtype=jnp.int32)
-    energy = energy_parts(velocity, magnetic, own, degrees)
     vmem = pl.BlockSpec(memory_space=pltpu.VMEM)
     hbm = pl.BlockSpec(memory_space=pl.ANY)
     dims = (rads, harm, shells, groups, modes, degrees, thetas, points)
@@ -726,7 +735,7 @@
         functools.partial(relay_kernel, dims),
         name="dynamo",
         out_shape=(result, result, jax.ShapeDtypeStruct((2, shells, degrees), F32)),
-        in_specs=[hbm] * 4 + [vmem] * 7,
+        in_specs=[hbm] * 4 + [vmem] * 6,
         out_specs=(vmem, vmem, vmem),
         scratch_shapes=[
             pltpu.VMEM((degrees, degrees, width), BF),
@@ -746,7 +755,8 @@
             pltpu.VMEM((shells, 12, modes, degrees), BF),
             pltpu.VMEM((2, 6, modes, degrees), BF),
             pltpu.VMEM((harm, 2, shells, degrees), F32),
-            dma((4,)), dma((shells, 4)), dma((shells, 4)), dma((shells, 4)), dma((shells, 4)),
+            pltpu.VMEM((2,) + velocity.shape, BF),
+            dma((4,)), dma((2,)), dma((shells, 4)), dma((shells, 4)), dma((shells, 4)), dma((shells, 4)),
             dma((shells,)), dma((shells,)), dma((shells,)), dma((shells,)),
             dma((2,)), dma((2,)), dma((harm,)), dma((harm,)),
         ],
@@ -754,14 +764,14 @@
             collective_id=0, has_side_effects=True, vmem_limit_bytes=62 * 1024 * 1024
         ),
     )(velocity, magnetic, vorticity, current, jnp.asarray(x), jnp.asarray(sect), jnp.asarray(unscale),
-      jnp.asarray(w), jnp.asarray(synthesis), jnp.asarray(analysis), energy)
+      jnp.asarray(w), jnp.asarray(synthesis), jnp.asarray(analysis))
 
 
 def relay_fits(mesh, args):
     _, total, _, degrees, _ = args[0].shape
     rads, harm = mesh.shape["rad"], mesh.shape["harm"]
     shells, modes = total // rads, degrees // harm
-    return harm == 2 * shells and rads > 2 and modes % 32 == 0 and degrees % (2 * LANES) == 0
+    return harm == 2 * shells and rads > 2 and rads % 2 == 0 and modes % 32 == 0 and degrees % (2 * LANES) == 0
 
 
 def solution(mesh):

time: 86.2 us -> 74.8 us (0.87)
  Pallas kernels: 80.1 us -> 70.8 us
  other arithmetic: 2.05 us -> 0 us
    pallas_call x1, Pallas kernels: 80.1 us -> 70.8 us  [local_relay(): pl.pallas_call(functools.partial(relay_kernel, dims), name='dynamo', out_...]
    reduce_sum x1 -> x0, other arithmetic: 1.34 us -> none  [energy_parts(): jnp.sum(field.astype(F32) ** 2 * energy_weight[None, None], axis=(0, 2, 3))]
where the time goes in v1:
time: 74.8 us; the launch traced here: 74.6 us
  Pallas kernels  70.8 us (95%)
  local copies, waits for them, and re-layouts  3.17 us (4%)
    pallas_call x1, Pallas kernels, local_relay(): pl.pallas_call(functools.partial(relay_kernel, dims), name='dynamo', out_...  70.8 us
    unnamed x7, local copies, waits for them, and re-layouts  3.17 us

profile of v1, /device:TPU:8, one launch (start us, length us, event | category | flops | bytes accessed | tf_op | source)
XLA Modules:
  0.0 74.6 jit_solution(12753945797903228431)
XLA Ops:
  0.6 70.8 %dynamo.1 = (bf16[3,4,2,32,256]{4,3,2,1,0:T(8,128)(2,1)}, bf16[3,4,2,32,256]{4,3,2,1,0:T(8,128)(2,1)}, f32[2,4,256]{2,1,0:T(4,128)}) custom-call(bf16[3,4,2,32,256]{4,3,2,1,0:T(8,128)(2,1)} %vel_ref.1, bf16[3,4,2,32,256]{4,3,2,1,0:T(8,128)(2,1)} %mag_ref.1, bf16[3,4,2,32,256]{4,3,2,1,0:T(8,128)(2,1)} %vor_ref.1, bf16[3,4,2,32,256]{4,3,2,1,0:T(8,128)(2,1)} %cur_ref.1, ...), custom_call_target="tpu_custom_call" | custom-call | tf_op jit(solution)/shard_map/dynamo/pallas_call | solution.py:734
  71.4 0.0 copy-start
  71.4 1.8 %copy.16 = bf16[3,4,2,32,256]{4,3,2,1,0:T(8,128)(2,1)} copy(bf16[3,4,2,32,256]{4,3,2,1,0:T(8,128)(2,1)} %get-tuple-element.6) | data formatting | bytes 786432
  73.3 0.0 copy-done
  73.3 0.0 copy-start.1
  73.3 0.7 copy.17
  74.0 0.0 copy-done.1
  74.0 0.6 copy.18
Async XLA Ops:
  71.4 1.8 %copy-start = (bf16[3,4,2,32,256]{4,3,2,1,0:T(8,128)(2,1)S(1)}, bf16[3,4,2,32,256]{4,3,2,1,0:T(8,128)(2,1)}, u32[]{:S(2)}) copy-start(bf16[3,4,2,32,256]{4,3,2,1,0:T(8,128)(2,1)} %get-tuple-element.7) | copy-start | bytes 1179652
  73.3 0.8 %copy-start.1 = (f32[2,4,256]{2,1,0:T(4,128)S(1)}, f32[2,4,256]{2,1,0:T(4,128)}, u32[]{:S(2)}) copy-start(f32[2,4,256]{2,1,0:T(4,128)} %get-tuple-element.8) | copy-start | bytes 24580

commit v2 on v1

--- a/solution.py
+++ b/solution.py
@@ -342,10 +342,10 @@
 
 def relay_kernel(
     dims,
-    vel_ref, mag_ref, vor_ref, cur_ref, x_ref, sect_ref, unscale_ref, w_ref, trig_ref, back_ref,
-    adv_ref, grad_ref, energy_out,
-    tab, rows, rx, cs, outs, modes_buf, grid, prod, asc, souts, own, ysend, yrecv, zsend, land, halo, energy_all, held,
-    lsem, vsem, zss, zrs, rss, rrs, yss, yrs, bss, brs, hss, hrs, esend, erecv,
+    vel_ref, mag_ref, vor_ref, cur_ref, x_hbm, sect_hbm, unscale_hbm, w_hbm, trig_hbm, back_hbm,
+    land_out, halo_out, energy_out,
+    x_ref, sect_ref, unscale_ref, w_ref, trig_ref, back_ref, tab, rows, rx, cs, outs, modes_buf, grid, prod, asc, souts, own, ysend, yrecv, zsend, land, halo, energy_all, held,
+    csem, osem, lsem, vsem, zss, zrs, rss, rrs, yss, yrs, bss, brs, hss, hrs, esend, erecv,
 ):
     rads, harm, shells, groups, modes, degrees, thetas, points = dims
     me = lax.axis_index("harm")
@@ -403,6 +403,13 @@
     def held_copy(f):
         return pltpu.make_async_copy(fields[f], held.at[f], vsem.at[f])
 
+    consts = [
+        pltpu.make_async_copy(src, dst, csem.at[i]) for i, (src, dst) in enumerate((
+            (x_hbm.at[core], x_ref), (sect_hbm.at[core], sect_ref), (unscale_hbm.at[core], unscale_ref),
+            (w_hbm.at[core], w_ref), (trig_hbm, trig_ref), (back_hbm, back_ref)))
+    ]
+    for copy in consts:
+        copy.start()
     for f in range(2):
         held_copy(f).start()
 
@@ -449,7 +456,9 @@
 
             relay(f, source, core).start()
 
-    x = x_ref[core, 0:1, :]
+    for copy in consts[:3]:
+        copy.wait()
+    x = x_ref[0:1, :]
     width = x.shape[1]
     per = 16
 
@@ -475,8 +484,8 @@
                 root = jnp.where(live, root, 0.0)
             new = guess * (x * latest - inverse * before)
             if starting:
-                new = new + jnp.where(lf == order, sect_ref[core, pl.ds(first, block), :], 0.0)
-            rows[inner] = new * unscale_ref[core, pl.ds(first, block), :]
+                new = new + jnp.where(lf == order, sect_ref[pl.ds(first, block), :], 0.0)
+            rows[inner] = new * unscale_ref[pl.ds(first, block), :]
             before, latest = latest, new
             inverse = root
         here = pl.ds(pl.multiple_of(step * per, per), per)
@@ -549,19 +558,27 @@
             relay(f, source, other).wait_recv()
         transform(source * groups + other, low_half[source])
 
+    def own_block(source):
+        transform(source * groups + core, low_half[source])
+
     for source in reversed(range(shells)):
         pass_on(source)
-        if source + 1 < shells:
+        if source + 1 < shells and (source < shells // 2 - 1 or source >= shells // 2):
             partner_block(source + 1)
-        transform(source * groups + core, low_half[source])
+        own_block(source)
+        if source == shells // 2:
+            partner_block(source)
     partner_block(0)
+
+    for copy in consts[3:]:
+        copy.wait()
 
     def synth(c, _):
         for par in range(2):
             grid[par, c] = jnp.dot(trig_ref[par], modes_buf[par, c], preferred_element_type=F32)
         return 0
 
-    lax.fori_loop(0, 12, synth, 0)
+    lax.fori_loop(0, 12, synth, 0, unroll=True)
 
     piece = 16
 
@@ -585,7 +602,7 @@
     def analyse(c, _):
         for par in range(2):
             a = jnp.dot(back_ref[par], prod[par, c], preferred_element_type=F32)
-            a = a * w_ref[core, 0:1, :]
+            a = a * w_ref[0:1, :]
             plus, minus = a[:, :width] + a[:, width:], a[:, :width] - a[:, width:]
             for r in range(2):
                 cut = slice(r * top, (r + 1) * top)
@@ -593,7 +610,7 @@
                 asc[par, 16 + 2 * c + r] = minus[cut]
         return 0
 
-    lax.fori_loop(0, 6, analyse, 0)
+    lax.fori_loop(0, 6, analyse, 0, unroll=True)
 
     out_lane = lax.broadcasted_iota(jnp.int32, (16, degrees), 1) % 2
 
@@ -628,29 +645,31 @@
     def _():
         land[:, :, :, 0:top] = jnp.zeros((shells, 12, modes, top), BF)
 
+    def finish(target):
+        low = low_half[target]
+        cut = slice(0, degrees) if low else slice(top, degrees)
+        ycopy(target).wait_recv()
+        total = (own[target, :, :, cut] + yrecv[target, :, :, cut].astype(F32)).astype(BF)
+        stays = jnp.logical_and(straight, z == target)
+
+        @pl.when(stays)
+        def _():
+            land[target, :, :, cut] = total
+
+        @pl.when(jnp.logical_not(stays))
+        def _():
+            zsend[target, :, :, cut] = total
+            bcopy(target, z, low).start()
+
     for target in range(shells):
         low = low_half[target]
         cut = slice(0, degrees) if low else slice(top, degrees)
         ysend[target, :, :, cut] = spectrum(target * groups + other, low).astype(BF)
         ycopy(target).start()
+        if target > 0:
+            finish(target - 1)
         own[target, :, :, cut] = spectrum(target * groups + core, low)
-
-    for target in range(shells):
-        low = low_half[target]
-        cut = slice(0, degrees) if low else slice(top, degrees)
-        ycopy(target).wait_recv()
-        total = (own[target, :, :, cut] + yrecv[target, :, :, cut].astype(F32)).astype(BF)
-
-        stays = jnp.logical_and(straight, z == target)
-
-        @pl.when(stays)
-        def _():
-            land[target, :, :, cut] = total
-
-        @pl.when(jnp.logical_not(stays))
-        def _():
-            zsend[target, :, :, cut] = total
-            bcopy(target, z, low).start()
+    finish(shells - 1)
 
     def arrived(shell):
         for low in (True, False):
@@ -666,32 +685,31 @@
             device_id=rad_up if side == 0 else rad_down, device_id_type=MESH,
         )
 
+    def out_copy(shell):
+        return pltpu.make_async_copy(land.at[shell], land_out.at[shell], osem.at[shell])
+
+    def halo_copy(side):
+        return pltpu.make_async_copy(halo.at[side], halo_out.at[side], osem.at[shells + side])
+
     arrived(shells - 1)
     hcopy(0).start()
+    out_copy(shells - 1).start()
     arrived(0)
     hcopy(1).start()
-    for shell in range(1, shells - 1):
-        arrived(shell)
+    out_copy(0).start()
     for step in range(1, harm):
         energy_copy(step).wait_recv()
     energy_out[...] = jnp.sum(energy_all[...], axis=0)
+    for shell in range(1, shells - 1):
+        arrived(shell)
+        out_copy(shell).start()
+    for side in range(2):
+        hcopy(side).wait_recv()
+        halo_copy(side).start()
     for shell in range(shells):
-        for k in range(6):
-            adv_ref[k // 2, shell, k % 2] = land[shell, k]
-    hcopy(0).wait_recv()
-    hcopy(1).wait_recv()
-    for shell in range(shells):
-        for k in range(6):
-            if shell > 0:
-                before = land[shell - 1, 6 + k].astype(F32)
-            else:
-                before = jnp.where(rad > 0, halo[0, k].astype(F32), 0.0)
-            if shell < shells - 1:
-                after = land[shell + 1, 6 + k].astype(F32)
-            else:
-                after = jnp.where(rad < rads - 1, halo[1, k].astype(F32), 0.0)
-            grad_ref[k // 2, shell, k % 2] = ((after - before) * 0.5).astype(BF)
-
+        out_copy(shell).wait()
+    for side in range(2):
+        halo_copy(side).wait()
     hcopy(0).wait_send()
     hcopy(1).wait_send()
     for step in range(1, harm):
@@ -729,15 +747,21 @@
     vmem = pl.BlockSpec(memory_space=pltpu.VMEM)
     hbm = pl.BlockSpec(memory_space=pl.ANY)
     dims = (rads, harm, shells, groups, modes, degrees, thetas, points)
-    result = jax.ShapeDtypeStruct(velocity.shape, BF)
     dma = pltpu.SemaphoreType.DMA
-    return pl.pallas_call(
+    consts = (x, sect, unscale, w, synthesis, analysis)
+    landed, halo, energy = pl.pallas_call(
         functools.partial(relay_kernel, dims),
         name="dynamo",
-        out_shape=(result, result, jax.ShapeDtypeStruct((2, shells, degrees), F32)),
-        in_specs=[hbm] * 4 + [vmem] * 6,
-        out_specs=(vmem, vmem, vmem),
+        out_shape=(
+            jax.ShapeDtypeStruct((shells, 12, modes, degrees), BF),
+            jax.ShapeDtypeStruct((2, 6, modes, degrees), BF),
+            jax.ShapeDtypeStruct((2, shells, degrees), F32),
+        ),
+        in_specs=[hbm] * 10,
+        out_specs=(hbm, hbm, vmem),
         scratch_shapes=[
+            *(pltpu.VMEM(c.shape[1:], c.dtype) for c in consts[:4]),
+            *(pltpu.VMEM(c.shape, c.dtype) for c in consts[4:]),
             pltpu.VMEM((degrees, degrees, width), BF),
             pltpu.VMEM((16, block, width), F32),
             pltpu.VMEM((harm, 4, 3, 2, modes, degrees), BF),
@@ -756,15 +780,22 @@
             pltpu.VMEM((2, 6, modes, degrees), BF),
             pltpu.VMEM((harm, 2, shells, degrees), F32),
             pltpu.VMEM((2,) + velocity.shape, BF),
-            dma((4,)), dma((2,)), dma((shells, 4)), dma((shells, 4)), dma((shells, 4)), dma((shells, 4)),
+            dma((6,)), dma((shells + 2,)), dma((4,)), dma((2,)), dma((shells, 4)), dma((shells, 4)), dma((shells, 4)), dma((shells, 4)),
             dma((shells,)), dma((shells,)), dma((shells,)), dma((shells,)),
             dma((2,)), dma((2,)), dma((harm,)), dma((harm,)),
         ],
         compiler_params=pltpu.CompilerParams(
             collective_id=0, has_side_effects=True, vmem_limit_bytes=62 * 1024 * 1024
         ),
-    )(velocity, magnetic, vorticity, current, jnp.asarray(x), jnp.asarray(sect), jnp.asarray(unscale),
-      jnp.asarray(w), jnp.asarray(synthesis), jnp.asarray(analysis))
+    )(velocity, magnetic, vorticity, current, *(jnp.asarray(c) for c in consts))
+
+    spectra = landed.reshape(shells, 6, 2, modes, degrees).transpose(1, 0, 2, 3, 4)
+    rad = lax.axis_index("rad")
+    below = jnp.where(rad > 0, halo[0].astype(F32), 0.0).reshape(3, 1, 2, modes, degrees)
+    above = jnp.where(rad < rads - 1, halo[1].astype(F32), 0.0).reshape(3, 1, 2, modes, degrees)
+    rimmed = jnp.concatenate([below, spectra[3:].astype(F32), above], axis=1)
+    gradient = ((rimmed[:, 2:] - rimmed[:, :-2]) * 0.5).astype(BF)
+    return spectra[:3], gradient, energy
 
 
 def relay_fits(mesh, args):

time: 74.8 us -> 68.4 us (0.914)
  Pallas kernels: 70.8 us -> 64 us
  other arithmetic: 0 us -> 1.75 us
  local copies, waits for them, and re-layouts: 3.17 us -> 1.87 us
    pallas_call x1, Pallas kernels: 70.8 us -> 64 us  [local_relay(): pl.pallas_call(functools.partial(relay_kernel, dims), name='dynamo', out_...]
    unnamed x7 -> x5, local copies, waits for them, and re-layouts: 3.17 us -> 0.68 us
    convert_element_type x0 -> x2, other arithmetic: none -> 1.72 us  [the longest x1 0.87 us: local_relay(): gradient = ((rimmed[:, 2:] - rimmed[:, :-2]) * 0.5).astype(BF)]
    reshape x0 -> x1, local copies, waits for them, and re-layouts: none -> 1.2 us  [local_relay(): landed.reshape(shells, 6, 2, modes, degrees).transpose(1, 0, 2, 3, 4)]
where the time goes in v2:
time: 68.4 us; the launch traced here: 68.3 us
  Pallas kernels  64 us (94%)
  local copies, waits for them, and re-layouts  1.87 us (3%)
  other arithmetic  1.75 us (3%)
    pallas_call x1, Pallas kernels, local_relay(): pl.pallas_call(functools.partial(relay_kernel, dims), name='dynamo', out_...  64 us

profile of v2, /device:TPU:8, one launch (start us, length us, event | category | flops | bytes accessed | tf_op | source)
XLA Modules:
  0.0 68.3 jit_solution(14610789978167921806)
XLA Ops:
  0.6 64.0 %dynamo.1 = (bf16[4,12,32,256]{3,2,1,0:T(8,128)(2,1)}, bf16[2,6,32,256]{3,2,1,0:T(8,128)(2,1)}, f32[2,4,256]{2,1,0:T(4,128)}) custom-call(bf16[3,4,2,32,256]{4,3,2,1,0:T(8,128)(2,1)} %vel_ref.1, bf16[3,4,2,32,256]{4,3,2,1,0:T(8,128)(2,1)} %mag_ref.1, bf16[3,4,2,32,256]{4,3,2,1,0:T(8,128)(2,1)} %vor_ref.1, bf16[3,4,2,32,256]{4,3,2,1,0:T(8,128)(2,1)} %cur_ref.1, ...), custom_call_target="tpu_custom_call" | custom-call | tf_op jit(solution)/shard_map/dynamo/pallas_call | solution.py:752
  64.6 1.2 %copy.17 = bf16[4,6,2,32,256]{4,3,2,0,1:T(8,128)(2,1)S(1)} copy(bf16[4,6,2,32,256]{4,3,2,1,0:T(8,128)(2,1)} %bitcast.11) | data formatting | bytes 1572864 | tf_op jit(solution)/shard_map/reshape | solution.py:792
  65.8 0.0 copy-start
  65.8 0.8 %slice_convert_fusion = (f32[3,4,2,32,256]{4,3,2,1,0:T(8,128)S(1)}, bf16[3,4,2,32,256]{4,3,2,1,0:T(8,128)(2,1)}) fusion(bf16[6,4,2,32,256]{4,3,2,1,0:T(8,128)(2,1)S(1)} %bitcast.10), kind=kLoop, calls=%fused_computation.6 | loop fusion | flops 196608 | bytes 1966080 | tf_op jit(solution)/shard_map/convert_element_type | solution.py:796
  66.7 0.1 copy-done
  66.8 0.0 copy-start.1
  66.8 0.9 %fusion.2 = bf16[3,4,2,32,256]{4,3,2,1,0:T(8,128)(2,1)} fusion(f32[3,4,2,32,256]{4,3,2,1,0:T(8,128)S(1)} %get-tuple-element.9, f32[3,1,2,32,256]{4,3,2,1,0:T(8,128)S(1)} %bitcast.13, f32[3,1,2,32,256]{4,3,2,1,0:T(8,128)S(1)} %bitcast.12), kind=kLoop, calls=%fused_computation.3 | loop fusion | flops 983040 | bytes 1572864 | tf_op jit(solution)/shard_map/convert_element_type | solution.py:797
  67.7 0.0 copy-done.1
  67.7 0.6 copy.19
  (1 shorter events, 0.0 us)
Async XLA Ops:
  65.8 0.9 %copy-start = (bf16[2,6,32,256]{3,2,1,0:T(8,128)(2,1)S(1)}, bf16[2,6,32,256]{3,2,1,0:T(8,128)(2,1)}, u32[]{:S(2)}) copy-start(bf16[2,6,32,256]{3,2,1,0:T(8,128)(2,1)} %get-tuple-element.7) | copy-start | bytes 589828
  66.8 0.9 %copy-start.1 = (f32[2,4,256]{2,1,0:T(4,128)S(1)}, f32[2,4,256]{2,1,0:T(4,128)}, u32[]{:S(2)}) copy-start(f32[2,4,256]{2,1,0:T(4,128)} %get-tuple-element.18) | copy-start | bytes 24580

commit v3 on v2

--- a/solution.py
+++ b/solution.py
@@ -343,9 +343,9 @@
 def relay_kernel(
     dims,
     vel_ref, mag_ref, vor_ref, cur_ref, x_hbm, sect_hbm, unscale_hbm, w_hbm, trig_hbm, back_hbm,
-    land_out, halo_out, energy_out,
+    land_out, halo_out, energy_hbm,
     x_ref, sect_ref, unscale_ref, w_ref, trig_ref, back_ref, tab, rows, rx, cs, outs, modes_buf, grid, prod, asc, souts, own, ysend, yrecv, zsend, land, halo, energy_all, held,
-    csem, osem, lsem, vsem, zss, zrs, rss, rrs, yss, yrs, bss, brs, hss, hrs, esend, erecv,
+    pack, rxp, zpack, landp, energy_out, csem, osem, lsem, vsem, zss, zrs, rss, rrs, yss, yrs, bss, brs, hss, hrs, esend, erecv, pss, prs, qss, qrs, bps, bpr,
 ):
     rads, harm, shells, groups, modes, degrees, thetas, points = dims
     me = lax.axis_index("harm")
@@ -358,6 +358,10 @@
     top = degrees // 2
     fields = (vel_ref, mag_ref, vor_ref, cur_ref)
     low_half = [src * block < top for src in range(shells)]
+    packed = [2 * src * block == top for src in range(shells)]
+    whole = [low and not half for low, half in zip(low_half, packed)]
+    mid = top // 2
+    packs = 2 * z * block == top
 
     def mate(shell):
         return {"rad": base + y, "harm": shell * groups + core}
@@ -390,10 +394,24 @@
         )
 
     def relay(f, source, yy):
-        slot = rx.at[source * groups + yy, f, :, :, :, lanes(low_half[source])]
+        slot = rx.at[source * groups + yy, f, :, :, :, lanes(whole[source])]
         return pltpu.make_async_remote_copy(
             src_ref=slot, dst_ref=slot,
             send_sem=rss.at[source, f], recv_sem=rrs.at[source, f],
+            device_id=partner, device_id_type=MESH,
+        )
+
+    def pcopy(f, dest, source):
+        return pltpu.make_async_remote_copy(
+            src_ref=pack.at[f, :, dest], dst_ref=rxp.at[y, f],
+            send_sem=pss.at[dest, f], recv_sem=prs.at[f],
+            device_id=mate(dest), device_id_type=MESH,
+        )
+
+    def relay_packed(f, yy):
+        return pltpu.make_async_remote_copy(
+            src_ref=rxp.at[yy, f], dst_ref=rxp.at[yy, f],
+            send_sem=qss.at[f], recv_sem=qrs.at[f],
             device_id=partner, device_id_type=MESH,
         )
 
@@ -424,17 +442,60 @@
         mark = shells - 1 - j
         return mark - jnp.where(mark <= z, 1, 0)
 
-    for low in (True, False):
-        @pl.when((z * block < top) == low)
-        def _(low=low):
-            for j in range(shells - 1):
-                for f in range(4):
-                    zcopy(f, dest_of(j), low, z).start()
-
+    is_whole = jnp.logical_and(z * block < top, jnp.logical_not(packs))
+
+    def routed(phase, send):
+        for j in range(shells - 1):
+            if j == 0:
+                if phase == 0:
+                    send(dest_of(j))
+            else:
+                crossing = jnp.logical_and(z * block < top, dest_of(j) * block >= top)
+
+                @pl.when(crossing == (phase == 1))
+                def _(j=j):
+                    send(dest_of(j))
+        if phase == 0:
             @pl.when(jnp.logical_not(straight))
             def _():
-                for f in range(4):
-                    zcopy(f, z, low, z).start()
+                send(z)
+
+    def plain_sends(phase, act, early=None):
+        for low in (True, False):
+            if early is not None and early == low:
+                continue
+
+            @pl.when(is_whole == low)
+            def _(low=low):
+                routed(phase, lambda dest: [act(zcopy(f, dest, low, z)) for f in range(4)])
+
+    def packed_sends(phase, act):
+        @pl.when(packs)
+        def _():
+            routed(phase, lambda dest: [act(pcopy(f, dest, z)) for f in range(4)])
+
+    def begin(copy):
+        copy.start()
+
+    plain_sends(0, begin)
+
+    @pl.when(packs)
+    def _():
+        for f in range(2, 4):
+            held_copy(f).start()
+        for f in range(4):
+            held_copy(f).wait()
+            for c in range(3):
+                for shell in range(shells):
+                    first, second = held[f, c, shell, 0, :, 0:top], held[f, c, shell, 1, :, 0:top]
+                    pack[f, c, shell] = jnp.concatenate([second[:, mid:], first[:, mid:]], axis=1)
+
+        @pl.when(straight)
+        def _():
+            for f in range(4):
+                rxp[core, f] = pack[f, :, z]
+
+    packed_sends(0, begin)
 
     def energy_copy(step):
         peer = lax.rem(me + step, harm)
@@ -452,9 +513,13 @@
 
             @pl.when(jnp.logical_not(jnp.logical_and(straight, z == source)))
             def _(f=f):
-                zcopy(f, source, low_half[source], source).wait_recv()
+                zcopy(f, source, whole[source], source).wait_recv()
+                if packed[source]:
+                    pcopy(f, source, source).wait_recv()
 
             relay(f, source, core).start()
+            if packed[source]:
+                relay_packed(f, core).start()
 
     for copy in consts[:3]:
         copy.wait()
@@ -507,10 +572,21 @@
     steps = degrees // per
     for source in reversed(range(shells)):
         carry = table_start(source)
-        lax.fori_loop((source + 1) * block // per, steps, functools.partial(table_block, source, False), carry)
-
-    for f in range(2):
-        held_copy(f).wait()
+        first = (source + 1) * block // per
+        turn = first + (steps - first) // 4 if source == 0 else steps
+        carry = lax.fori_loop(first, turn, functools.partial(table_block, source, False), carry)
+        if source == 1:
+            plain_sends(1, begin, early=True)
+            packed_sends(1, begin)
+        if source == 0:
+            plain_sends(1, begin, early=False)
+            lax.fori_loop(turn, steps, functools.partial(table_block, source, False), carry)
+
+    @pl.when(jnp.logical_not(packs))
+    def _():
+        for f in range(2):
+            held_copy(f).wait()
+
     own_order = me * modes + lax.broadcasted_iota(jnp.int32, (modes, degrees), 0)
     degree = lax.broadcasted_iota(jnp.int32, (modes, degrees), 1)
     share = jnp.where(degree >= own_order, 1.0 / (2.0 * degree.astype(F32) + 1.0), 0.0)
@@ -535,10 +611,17 @@
     lane = lax.broadcasted_iota(jnp.int32, (24, degrees), 1) % 2
     half_modes = modes // 2
 
-    def transform(b, low):
-        cut = slice(0, degrees) if low else slice(top, degrees)
-        cs[:, :, cut] = jnp.swapaxes(
-            rx[b].reshape(24, modes, degrees)[:, :, cut].astype(F32), 0, 1)
+    def transform(source, yy):
+        b = source * groups + yy
+        cut = slice(0, degrees) if low_half[source] else slice(top, degrees)
+        direct = slice(0, degrees) if whole[source] else slice(top, degrees)
+        cs[:, :, direct] = jnp.swapaxes(
+            rx[b].reshape(24, modes, degrees)[:, :, direct].astype(F32), 0, 1)
+        if packed[source]:
+            first = rxp[yy].reshape(12, 1, modes, top).astype(F32)
+            second = jnp.concatenate([first[..., mid:], first[..., :mid]], axis=3)
+            both = jnp.concatenate([first, second], axis=1).reshape(24, modes, top)
+            cs[:, :, 0:top] = jnp.swapaxes(both, 0, 1)
         for par in range(2):
             for i in range(half_modes):
                 c = cs[2 * i + par, :, cut]
@@ -556,19 +639,25 @@
     def partner_block(source):
         for f in range(4):
             relay(f, source, other).wait_recv()
-        transform(source * groups + other, low_half[source])
+            if packed[source]:
+                relay_packed(f, other).wait_recv()
+        transform(source, other)
 
     def own_block(source):
-        transform(source * groups + core, low_half[source])
-
-    for source in reversed(range(shells)):
+        transform(source, core)
+
+    near = list(reversed(range(shells // 2, shells)))
+    far = list(range(shells // 2))
+    for i, source in enumerate(near):
         pass_on(source)
-        if source + 1 < shells and (source < shells // 2 - 1 or source >= shells // 2):
-            partner_block(source + 1)
+        if i > 0:
+            partner_block(near[i - 1])
         own_block(source)
-        if source == shells // 2:
-            partner_block(source)
-    partner_block(0)
+    partner_block(near[-1])
+    for source in far:
+        pass_on(source)
+        own_block(source)
+        partner_block(source)
 
     for copy in consts[3:]:
         copy.wait()
@@ -636,57 +725,82 @@
 
     def bcopy(target, shell, low):
         return pltpu.make_async_remote_copy(
-            src_ref=zsend.at[target, :, :, lanes(low)], dst_ref=land.at[shell, :, :, lanes(low)],
+            src_ref=zsend.at[target, :, :, :, lanes(low)], dst_ref=land.at[shell, :, :, :, lanes(low)],
             send_sem=bss.at[target], recv_sem=brs.at[shell],
             device_id=mate(target), device_id_type=MESH,
         )
 
+    def bpack(target, shell):
+        return pltpu.make_async_remote_copy(
+            src_ref=zpack, dst_ref=landp.at[shell],
+            send_sem=bps.at[0], recv_sem=bpr.at[shell],
+            device_id=mate(target), device_id_type=MESH,
+        )
+
     @pl.when(z * block >= top)
     def _():
-        land[:, :, :, 0:top] = jnp.zeros((shells, 12, modes, top), BF)
+        land[:, :, :, :, 0:top] = jnp.zeros((shells, 6, 2, modes, top), BF)
 
     def finish(target):
         low = low_half[target]
         cut = slice(0, degrees) if low else slice(top, degrees)
         ycopy(target).wait_recv()
         total = (own[target, :, :, cut] + yrecv[target, :, :, cut].astype(F32)).astype(BF)
+        total = total.reshape(6, 2, modes, total.shape[-1])
         stays = jnp.logical_and(straight, z == target)
 
         @pl.when(stays)
         def _():
-            land[target, :, :, cut] = total
+            land[target, :, :, :, cut] = total
 
         @pl.when(jnp.logical_not(stays))
         def _():
-            zsend[target, :, :, cut] = total
-            bcopy(target, z, low).start()
+            zsend[target, :, :, :, cut] = total
+            bcopy(target, z, whole[target]).start()
+            if packed[target]:
+                zpack[...] = jnp.concatenate([total[:, 1, :, mid:top], total[:, 0, :, mid:top]], axis=2)
+                bpack(target, z).start()
 
     for target in range(shells):
         low = low_half[target]
         cut = slice(0, degrees) if low else slice(top, degrees)
         ysend[target, :, :, cut] = spectrum(target * groups + other, low).astype(BF)
         ycopy(target).start()
-        if target > 0:
+        if target > 1:
             finish(target - 1)
         own[target, :, :, cut] = spectrum(target * groups + core, low)
+        if target == 0:
+            finish(0)
     finish(shells - 1)
 
+    upper = lax.broadcasted_iota(jnp.int32, (modes, top), 1) >= mid
+
     def arrived(shell):
+        moved = jnp.logical_not(jnp.logical_and(straight, z == shell))
         for low in (True, False):
-            @pl.when(jnp.logical_and(jnp.logical_not(jnp.logical_and(straight, z == shell)), (z * block < top) == low))
+            @pl.when(jnp.logical_and(moved, is_whole == low))
             def _(low=low):
                 bcopy(shell, shell, low).wait_recv()
 
+        @pl.when(jnp.logical_and(moved, packs))
+        def _():
+            bpack(shell, shell).wait_recv()
+            for k in range(6):
+                first = landp[shell, k].astype(F32)
+                second = jnp.concatenate([first[:, mid:], first[:, :mid]], axis=1)
+                land[shell, k, 0, :, 0:top] = jnp.where(upper, first, 0.0).astype(BF)
+                land[shell, k, 1, :, 0:top] = jnp.where(upper, second, 0.0).astype(BF)
+
     def hcopy(side):
         shell = shells - 1 if side == 0 else 0
         return pltpu.make_async_remote_copy(
-            src_ref=land.at[shell, pl.ds(6, 6)], dst_ref=halo.at[side],
+            src_ref=land.at[shell, pl.ds(3, 3)], dst_ref=halo.at[side],
             send_sem=hss.at[side], recv_sem=hrs.at[side],
             device_id=rad_up if side == 0 else rad_down, device_id_type=MESH,
         )
 
     def out_copy(shell):
-        return pltpu.make_async_copy(land.at[shell], land_out.at[shell], osem.at[shell])
+        return pltpu.make_async_copy(land.at[shell], land_out.at[:, shell], osem.at[shell])
 
     def halo_copy(side):
         return pltpu.make_async_copy(halo.at[side], halo_out.at[side], osem.at[shells + side])
@@ -700,6 +814,8 @@
     for step in range(1, harm):
         energy_copy(step).wait_recv()
     energy_out[...] = jnp.sum(energy_all[...], axis=0)
+    energy_done = pltpu.make_async_copy(energy_out, energy_hbm, osem.at[shells + 2])
+    energy_done.start()
     for shell in range(1, shells - 1):
         arrived(shell)
         out_copy(shell).start()
@@ -710,30 +826,29 @@
         out_copy(shell).wait()
     for side in range(2):
         halo_copy(side).wait()
+    energy_done.wait()
     hcopy(0).wait_send()
     hcopy(1).wait_send()
     for step in range(1, harm):
         energy_copy(step).wait_send()
-    for low in (True, False):
-        @pl.when((z * block < top) == low)
-        def _(low=low):
-            for j in range(shells - 1):
-                for f in range(4):
-                    zcopy(f, dest_of(j), low, z).wait_send()
-
-            @pl.when(jnp.logical_not(straight))
-            def _():
-                for f in range(4):
-                    zcopy(f, z, low, z).wait_send()
-
+    def ended(copy):
+        copy.wait_send()
+
+    for phase in range(2):
+        plain_sends(phase, ended)
+        packed_sends(phase, ended)
     for source in range(shells):
         for f in range(4):
             relay(f, source, core).wait_send()
+            if packed[source]:
+                relay_packed(f, core).wait_send()
         ycopy(source).wait_send()
 
         @pl.when(jnp.logical_not(jnp.logical_and(straight, z == source)))
         def _(source=source):
-            bcopy(source, z, low_half[source]).wait_send()
+            bcopy(source, z, whole[source]).wait_send()
+            if packed[source]:
+                bpack(source, z).wait_send()
 
 
 def local_relay(velocity, magnetic, vorticity, current):
@@ -744,7 +859,6 @@
     x, sect, unscale, w, synthesis, analysis = relay_tables(degrees, thetas, points, groups)
     width = x.shape[2]
     block = groups * modes
-    vmem = pl.BlockSpec(memory_space=pltpu.VMEM)
     hbm = pl.BlockSpec(memory_space=pl.ANY)
     dims = (rads, harm, shells, groups, modes, degrees, thetas, points)
     dma = pltpu.SemaphoreType.DMA
@@ -753,12 +867,12 @@
         functools.partial(relay_kernel, dims),
         name="dynamo",
         out_shape=(
-            jax.ShapeDtypeStruct((shells, 12, modes, degrees), BF),
-            jax.ShapeDtypeStruct((2, 6, modes, degrees), BF),
+            jax.ShapeDtypeStruct((6, shells, 2, modes, degrees), BF),
+            jax.ShapeDtypeStruct((2, 3, 2, modes, degrees), BF),
             jax.ShapeDtypeStruct((2, shells, degrees), F32),
         ),
         in_specs=[hbm] * 10,
-        out_specs=(hbm, hbm, vmem),
+        out_specs=(hbm, hbm, hbm),
         scratch_shapes=[
             *(pltpu.VMEM(c.shape[1:], c.dtype) for c in consts[:4]),
             *(pltpu.VMEM(c.shape, c.dtype) for c in consts[4:]),
@@ -775,27 +889,32 @@
             pltpu.VMEM((shells, 12, modes, degrees), F32),
             pltpu.VMEM((shells, 12, modes, degrees), BF),
             pltpu.VMEM((shells, 12, modes, degrees), BF),
-            pltpu.VMEM((shells, 12, modes, degrees), BF),
-            pltpu.VMEM((shells, 12, modes, degrees), BF),
-            pltpu.VMEM((2, 6, modes, degrees), BF),
+            pltpu.VMEM((shells, 6, 2, modes, degrees), BF),
+            pltpu.VMEM((shells, 6, 2, modes, degrees), BF),
+            pltpu.VMEM((2, 3, 2, modes, degrees), BF),
             pltpu.VMEM((harm, 2, shells, degrees), F32),
-            pltpu.VMEM((2,) + velocity.shape, BF),
-            dma((6,)), dma((shells + 2,)), dma((4,)), dma((2,)), dma((shells, 4)), dma((shells, 4)), dma((shells, 4)), dma((shells, 4)),
+            pltpu.VMEM((4,) + velocity.shape, BF),
+            pltpu.VMEM((4, 3, shells, modes, degrees // 2), BF),
+            pltpu.VMEM((groups, 4, 3, modes, degrees // 2), BF),
+            pltpu.VMEM((6, modes, degrees // 2), BF),
+            pltpu.VMEM((shells, 6, modes, degrees // 2), BF),
+            pltpu.VMEM((2, shells, degrees), F32),
+            dma((6,)), dma((shells + 3,)), dma((4,)), dma((4,)), dma((shells, 4)), dma((shells, 4)), dma((shells, 4)), dma((shells, 4)),
             dma((shells,)), dma((shells,)), dma((shells,)), dma((shells,)),
             dma((2,)), dma((2,)), dma((harm,)), dma((harm,)),
+            dma((shells, 4)), dma((4,)), dma((4,)), dma((4,)), dma((1,)), dma((shells,)),
         ],
         compiler_params=pltpu.CompilerParams(
             collective_id=0, has_side_effects=True, vmem_limit_bytes=62 * 1024 * 1024
         ),
     )(velocity, magnetic, vorticity, current, *(jnp.asarray(c) for c in consts))
 
-    spectra = landed.reshape(shells, 6, 2, modes, degrees).transpose(1, 0, 2, 3, 4)
     rad = lax.axis_index("rad")
     below = jnp.where(rad > 0, halo[0].astype(F32), 0.0).reshape(3, 1, 2, modes, degrees)
     above = jnp.where(rad < rads - 1, halo[1].astype(F32), 0.0).reshape(3, 1, 2, modes, degrees)
-    rimmed = jnp.concatenate([below, spectra[3:].astype(F32), above], axis=1)
+    rimmed = jnp.concatenate([below, landed[3:].astype(F32), above], axis=1)
     gradient = ((rimmed[:, 2:] - rimmed[:, :-2]) * 0.5).astype(BF)
-    return spectra[:3], gradient, energy
+    return landed[:3], gradient, energy
 
 
 def relay_fits(mesh, args):

time: 68.4 us -> 61.2 us (0.89)
  Pallas kernels: 64 us -> 56.7 us
  local copies, waits for them, and re-layouts: 1.87 us -> 0.61 us
  other arithmetic: 1.75 us -> 2.91 us
    pallas_call x1, Pallas kernels: 64 us -> 56.7 us  [local_relay(): pl.pallas_call(functools.partial(relay_kernel, dims), name='dynamo', out_...]
    reshape x1 -> x0, local copies, waits for them, and re-layouts: 1.2 us -> none  [local_relay(): landed.reshape(shells, 6, 2, modes, degrees).transpose(1, 0, 2, 3, 4)]
    convert_element_type x1, other arithmetic: 0.85 us -> 2 us  [local_relay(): rimmed = jnp.concatenate([below, landed[3:].astype(F32), above], axis=1)]
where the time goes in v3:
time: 61.2 us; the launch traced here: 60.9 us
  Pallas kernels  56.7 us (93%)
  other arithmetic  2.91 us (5%)
  between operations  0.67 us (1%)
    pallas_call x1, Pallas kernels, local_relay(): pl.pallas_call(functools.partial(relay_kernel, dims), name='dynamo', out_...  56.7 us
    convert_element_type x1, other arithmetic, local_relay(): rimmed = jnp.concatenate([below, landed[3:].astype(F32), above], axis=1)  2 us

profile of v3, /device:TPU:8, one launch (start us, length us, event | category | flops | bytes accessed | tf_op | source)
XLA Modules:
  0.0 60.9 jit_solution(16545882698189783031)
XLA Ops:
  0.6 56.7 %dynamo.1 = (bf16[6,4,2,32,256]{4,3,2,1,0:T(8,128)(2,1)}, bf16[2,3,2,32,256]{4,3,2,1,0:T(8,128)(2,1)}, f32[2,4,256]{2,1,0:T(4,128)}) custom-call(bf16[3,4,2,32,256]{4,3,2,1,0:T(8,128)(2,1)} %vel_ref.1, bf16[3,4,2,32,256]{4,3,2,1,0:T(8,128)(2,1)} %mag_ref.1, bf16[3,4,2,32,256]{4,3,2,1,0:T(8,128)(2,1)} %vor_ref.1, bf16[3,4,2,32,256]{4,3,2,1,0:T(8,128)(2,1)} %cur_ref.1, ...), custom_call_target="tpu_custom_call" | custom-call | tf_op jit(solution)/shard_map/dynamo/pallas_call | solution.py:866
  57.4 0.0 copy-start
  57.4 2.0 %slice_convert_fusion = (f32[3,4,2,32,256]{4,3,2,1,0:T(8,128)S(1)}, bf16[3,4,2,32,256]{4,3,2,1,0:T(8,128)(2,1)}) fusion(bf16[6,4,2,32,256]{4,3,2,1,0:T(8,128)(2,1)} %get-tuple-element.6), kind=kLoop, calls=%fused_computation.5 | loop fusion | flops 196608 | bytes 1966080 | tf_op jit(solution)/shard_map/convert_element_type | solution.py:915
  59.4 0.0 copy-done
  59.4 0.0 copy-start.1
  59.5 0.9 %fusion.2 = bf16[3,4,2,32,256]{4,3,2,1,0:T(8,128)(2,1)} fusion(f32[3,4,2,32,256]{4,3,2,1,0:T(8,128)S(1)} %get-tuple-element.9, f32[3,1,2,32,256]{4,3,2,1,0:T(8,128)S(1)} %get-tuple-element.12, f32[3,1,2,32,256]{4,3,2,1,0:T(8,128)S(1)} %get-tuple-element.11), kind=kLoop, calls=%fused_computation.3 | loop fusion | flops 983040 | bytes 1572864 | tf_op jit(solution)/shard_map/convert_element_type | solution.py:916
  60.3 0.0 copy-done.1
  60.3 0.6 copy.16
  (1 shorter events, 0.0 us)
Async XLA Ops:
  57.4 2.0 %copy-start = (bf16[2,3,2,32,256]{4,3,2,1,0:T(8,128)(2,1)S(1)}, bf16[2,3,2,32,256]{4,3,2,1,0:T(8,128)(2,1)}, u32[]{:S(2)}) copy-start(bf16[2,3,2,32,256]{4,3,2,1,0:T(8,128)(2,1)} %get-tuple-element.7) | copy-start | bytes 589828
  59.4 0.9 %copy-start.1 = (f32[2,4,256]{2,1,0:T(4,128)S(1)}, f32[2,4,256]{2,1,0:T(4,128)}, u32[]{:S(2)}) copy-start(f32[2,4,256]{2,1,0:T(4,128)} %get-tuple-element.18) | copy-start | bytes 24580

commit v4 on v3

--- a/solution.py
+++ b/solution.py
@@ -662,18 +662,11 @@
     for copy in consts[3:]:
         copy.wait()
 
-    def synth(c, _):
-        for par in range(2):
-            grid[par, c] = jnp.dot(trig_ref[par], modes_buf[par, c], preferred_element_type=F32)
-        return 0
-
-    lax.fori_loop(0, 12, synth, 0, unroll=True)
-
     piece = 16
 
     def product_rows(i, _):
-        at_rows = pl.ds(pl.multiple_of((i // 2) * piece, piece), piece)
-        at_lanes = pl.ds(pl.multiple_of((i % 2) * width, width), width)
+        at_rows = pl.ds((i // 2) * piece, piece)
+        at_lanes = pl.ds((i % 2) * width, width)
         e = [grid[0, c, at_rows, at_lanes] for c in range(12)]
         o = [grid[1, c, at_rows, at_lanes] for c in range(12)]
         sides = []
@@ -686,7 +679,19 @@
             prod[1, c, at_rows, at_lanes] = (sides[0][c] - sides[1][c]).astype(BF)
         return 0
 
-    lax.fori_loop(0, points // 2 // piece * 2, product_rows, 0)
+
+    span = points // 2 // 3
+    for part in range(3):
+        at_part = slice(part * span, (part + 1) * span)
+        for c in range(12):
+            for par in range(2):
+                grid[par, c, at_part] = jnp.dot(
+                    trig_ref[par, at_part], modes_buf[par, c], preferred_element_type=F32)
+        if part > 0:
+            for i in range((part - 1) * span // piece * 2, part * span // piece * 2):
+                product_rows(i, 0)
+    for i in range(2 * span // piece * 2, 3 * span // piece * 2):
+        product_rows(i, 0)
 
     def analyse(c, _):
         for par in range(2):
@@ -703,8 +708,10 @@
 
     out_lane = lax.broadcasted_iota(jnp.int32, (16, degrees), 1) % 2
 
-    def spectrum(b, low):
-        cut = slice(0, degrees) if low else slice(top, degrees)
+    sides = (slice(0, top), slice(top, degrees), slice(0, degrees))
+
+    def spectrum(b, part):
+        cut = sides[part]
         for par in range(2):
             here = pl.ds(pl.multiple_of(b * half_modes, half_modes), half_modes)
             turned = jnp.swapaxes(asc[par, :, here, :], 0, 1).astype(BF)
@@ -715,18 +722,19 @@
                 souts[2 * i + par, :, cut] = jnp.where(out_lane[:, cut] == par, both[:16], both[16:])
         return jnp.swapaxes(souts[:, :, cut], 0, 1)[:12]
 
-    def ycopy(target):
-        low = low_half[target]
-        return pltpu.make_async_remote_copy(
-            src_ref=ysend.at[target, :, :, lanes(low)], dst_ref=yrecv.at[target, :, :, lanes(low)],
-            send_sem=yss.at[target], recv_sem=yrs.at[target],
+    def ycopy(target, part):
+        here = pl.ds(0, degrees) if part == 2 else pl.ds(part * top, top)
+        return pltpu.make_async_remote_copy(
+            src_ref=ysend.at[target, :, :, here], dst_ref=yrecv.at[target, :, :, here],
+            send_sem=yss.at[target, part % 2], recv_sem=yrs.at[target, part % 2],
             device_id=partner, device_id_type=MESH,
         )
 
-    def bcopy(target, shell, low):
-        return pltpu.make_async_remote_copy(
-            src_ref=zsend.at[target, :, :, :, lanes(low)], dst_ref=land.at[shell, :, :, :, lanes(low)],
-            send_sem=bss.at[target], recv_sem=brs.at[shell],
+    def bcopy(target, shell, part):
+        here = pl.ds(part * top, top)
+        return pltpu.make_async_remote_copy(
+            src_ref=zsend.at[target, :, :, :, here], dst_ref=land.at[shell, :, :, :, here],
+            send_sem=bss.at[target, part], recv_sem=brs.at[shell, part],
             device_id=mate(target), device_id_type=MESH,
         )
 
@@ -741,10 +749,17 @@
     def _():
         land[:, :, :, :, 0:top] = jnp.zeros((shells, 6, 2, modes, top), BF)
 
-    def finish(target):
-        low = low_half[target]
-        cut = slice(0, degrees) if low else slice(top, degrees)
-        ycopy(target).wait_recv()
+    def returned(target, part, shell):
+        copies = []
+        if part != 0:
+            copies.append(bcopy(target, shell, 1))
+        if part != 1:
+            copies.append(bpack(target, shell) if packed[target] else bcopy(target, shell, 0))
+        return copies
+
+    def finish(target, part):
+        cut = sides[part]
+        ycopy(target, part).wait_recv()
         total = (own[target, :, :, cut] + yrecv[target, :, :, cut].astype(F32)).astype(BF)
         total = total.reshape(6, 2, modes, total.shape[-1])
         stays = jnp.logical_and(straight, z == target)
@@ -756,31 +771,22 @@
         @pl.when(jnp.logical_not(stays))
         def _():
             zsend[target, :, :, :, cut] = total
-            bcopy(target, z, whole[target]).start()
-            if packed[target]:
+            if part != 1 and packed[target]:
                 zpack[...] = jnp.concatenate([total[:, 1, :, mid:top], total[:, 0, :, mid:top]], axis=2)
-                bpack(target, z).start()
-
-    for target in range(shells):
-        low = low_half[target]
-        cut = slice(0, degrees) if low else slice(top, degrees)
-        ysend[target, :, :, cut] = spectrum(target * groups + other, low).astype(BF)
-        ycopy(target).start()
-        if target > 1:
-            finish(target - 1)
-        own[target, :, :, cut] = spectrum(target * groups + core, low)
-        if target == 0:
-            finish(0)
-    finish(shells - 1)
+            for copy in returned(target, part, z):
+                copy.start()
 
     upper = lax.broadcasted_iota(jnp.int32, (modes, top), 1) >= mid
 
     def arrived(shell):
         moved = jnp.logical_not(jnp.logical_and(straight, z == shell))
-        for low in (True, False):
-            @pl.when(jnp.logical_and(moved, is_whole == low))
-            def _(low=low):
-                bcopy(shell, shell, low).wait_recv()
+        @pl.when(moved)
+        def _():
+            bcopy(shell, shell, 1).wait_recv()
+
+        @pl.when(jnp.logical_and(moved, is_whole))
+        def _():
+            bcopy(shell, shell, 0).wait_recv()
 
         @pl.when(jnp.logical_and(moved, packs))
         def _():
@@ -805,12 +811,27 @@
     def halo_copy(side):
         return pltpu.make_async_copy(halo.at[side], halo_out.at[side], osem.at[shells + side])
 
-    arrived(shells - 1)
-    hcopy(0).start()
-    out_copy(shells - 1).start()
-    arrived(0)
-    hcopy(1).start()
-    out_copy(0).start()
+    def edges_out():
+        arrived(shells - 1)
+        hcopy(0).start()
+        out_copy(shells - 1).start()
+        arrived(0)
+        hcopy(1).start()
+        out_copy(0).start()
+
+    late = z == shells // 2
+    pieces = [(0, 1), (0, 0)] + [(target, 2 if low_half[target] else 1) for target in range(1, shells)]
+    for i, (target, part) in enumerate(pieces):
+        ysend[target, :, :, sides[part]] = spectrum(target * groups + other, part).astype(BF)
+        ycopy(target, part).start()
+        if i > 0:
+            finish(*pieces[i - 1])
+        own[target, :, :, sides[part]] = spectrum(target * groups + core, part)
+        if i == len(pieces) - 2:
+            pl.when(late)(edges_out)
+    finish(*pieces[-1])
+    pl.when(jnp.logical_not(late))(edges_out)
+
     for step in range(1, harm):
         energy_copy(step).wait_recv()
     energy_out[...] = jnp.sum(energy_all[...], axis=0)
@@ -842,13 +863,49 @@
             relay(f, source, core).wait_send()
             if packed[source]:
                 relay_packed(f, core).wait_send()
-        ycopy(source).wait_send()
-
-        @pl.when(jnp.logical_not(jnp.logical_and(straight, z == source)))
-        def _(source=source):
-            bcopy(source, z, whole[source]).wait_send()
-            if packed[source]:
-                bpack(source, z).wait_send()
+
+    for target, part in pieces:
+        ycopy(target, part).wait_send()
+
+        @pl.when(jnp.logical_not(jnp.logical_and(straight, z == target)))
+        def _(target=target, part=part):
+            for copy in returned(target, part, z):
+                copy.wait_send()
+
+
+def closing_kernel(
+    rads, shells, landed, halo, energy, adv_out, grad_out, energy_out, adv, ind, grad, rim, total, isem, osem
+):
+    rad = lax.axis_index("rad")
+    copy = pltpu.make_async_copy
+    halos = copy(halo, rim, isem.at[0])
+    induced = [copy(landed.at[pl.ds(3, 3), s], ind.at[:, s], isem.at[3 + s]) for s in range(shells)]
+    advected = copy(landed.at[pl.ds(0, 3)], adv, isem.at[1])
+    energies = copy(energy, total, isem.at[2])
+    halos.start()
+    for shell in induced:
+        shell.start()
+    advected.start()
+    energies.start()
+    outs = [copy(grad.at[:, s], grad_out.at[:, s], osem.at[2 + s]) for s in range(shells)]
+    outs += [copy(adv, adv_out, osem.at[0]), copy(total, energy_out, osem.at[1])]
+    halos.wait()
+    induced[0].wait()
+    for s in range(shells):
+        if s + 1 < shells:
+            induced[s + 1].wait()
+            after = ind[:, s + 1].astype(F32)
+        else:
+            after = jnp.where(rad < rads - 1, rim[1].astype(F32), 0.0)
+        before = ind[:, s - 1].astype(F32) if s > 0 else jnp.where(rad > 0, rim[0].astype(F32), 0.0)
+        grad[:, s] = ((after - before) * 0.5).astype(BF)
+        outs[s].start()
+    advected.wait()
+    outs[shells].start()
+    energies.wait()
+    outs[shells + 1].start()
+    for out in outs:
+        out.wait()
 
 
 def local_relay(velocity, magnetic, vorticity, current):
@@ -900,7 +957,7 @@
             pltpu.VMEM((shells, 6, modes, degrees // 2), BF),
             pltpu.VMEM((2, shells, degrees), F32),
             dma((6,)), dma((shells + 3,)), dma((4,)), dma((4,)), dma((shells, 4)), dma((shells, 4)), dma((shells, 4)), dma((shells, 4)),
-            dma((shells,)), dma((shells,)), dma((shells,)), dma((shells,)),
+            dma((shells, 2)), dma((shells, 2)), dma((shells, 2)), dma((shells, 2)),
             dma((2,)), dma((2,)), dma((harm,)), dma((harm,)),
             dma((shells, 4)), dma((4,)), dma((4,)), dma((4,)), dma((1,)), dma((shells,)),
         ],
@@ -909,12 +966,22 @@
         ),
     )(velocity, magnetic, vorticity, current, *(jnp.asarray(c) for c in consts))
 
-    rad = lax.axis_index("rad")
-    below = jnp.where(rad > 0, halo[0].astype(F32), 0.0).reshape(3, 1, 2, modes, degrees)
-    above = jnp.where(rad < rads - 1, halo[1].astype(F32), 0.0).reshape(3, 1, 2, modes, degrees)
-    rimmed = jnp.concatenate([below, landed[3:].astype(F32), above], axis=1)
-    gradient = ((rimmed[:, 2:] - rimmed[:, :-2]) * 0.5).astype(BF)
-    return landed[:3], gradient, energy
+    half = (3,) + landed.shape[1:]
+    return pl.pallas_call(
+        functools.partial(closing_kernel, rads, shells),
+        name="closing",
+        out_shape=(
+            jax.ShapeDtypeStruct(half, BF),
+            jax.ShapeDtypeStruct(half, BF),
+            jax.ShapeDtypeStruct(energy.shape, F32),
+        ),
+        in_specs=[hbm] * 3,
+        out_specs=(hbm, hbm, hbm),
+        scratch_shapes=[
+            pltpu.VMEM(half, BF), pltpu.VMEM(half, BF), pltpu.VMEM(half, BF),
+            pltpu.VMEM(halo.shape, BF), pltpu.VMEM(energy.shape, F32), dma((5 + shells,)), dma((2 + shells,)),
+        ],
+    )(landed, halo, energy)
 
 
 def relay_fits(mesh, args):

time: 61.2 us -> 58.7 us (0.959)
  other arithmetic: 2.91 us -> 0 us
  Pallas kernels: 56.7 us -> 57.6 us
    convert_element_type x2 -> x0, other arithmetic: 2.88 us -> none  [the longest x1 2 us: local_relay(): rimmed = jnp.concatenate([below, landed[3:].astype(F32), above], axis=1)]
    pallas_call x0 -> x1, Pallas kernels: none -> 2.17 us  [local_relay(): pl.pallas_call(functools.partial(closing_kernel, rads, shells), name='clo...]
    pallas_call x1, Pallas kernels: 56.7 us -> 55.4 us  [local_relay(): pl.pallas_call(functools.partial(relay_kernel, dims), name='dynamo', out_...]
where the time goes in v4:
time: 58.7 us; the launch traced here: 58.4 us
  Pallas kernels  57.6 us (98%)
  between operations  0.8 us (1%)
    pallas_call x1, Pallas kernels, local_relay(): pl.pallas_call(functools.partial(relay_kernel, dims), name='dynamo', out_...  55.4 us
    pallas_call x1, Pallas kernels, local_relay(): pl.pallas_call(functools.partial(closing_kernel, rads, shells), name='clo...  2.17 us

profile of v4, /device:TPU:8, one launch (start us, length us, event | category | flops | bytes accessed | tf_op | source)
XLA Modules:
  0.0 58.4 jit_solution(10711015792703619120)
XLA Ops:
  0.6 55.4 %dynamo.1 = (bf16[6,4,2,32,256]{4,3,2,1,0:T(8,128)(2,1)}, bf16[2,3,2,32,256]{4,3,2,1,0:T(8,128)(2,1)}, f32[2,4,256]{2,1,0:T(4,128)}) custom-call(bf16[3,4,2,32,256]{4,3,2,1,0:T(8,128)(2,1)} %vel_ref.1, bf16[3,4,2,32,256]{4,3,2,1,0:T(8,128)(2,1)} %mag_ref.1, bf16[3,4,2,32,256]{4,3,2,1,0:T(8,128)(2,1)} %vor_ref.1, bf16[3,4,2,32,256]{4,3,2,1,0:T(8,128)(2,1)} %cur_ref.1, ...), custom_call_target="tpu_custom_call" | custom-call | tf_op jit(solution)/shard_map/dynamo/pallas_call | solution.py:923
  56.1 2.2 %closing.1 = (bf16[3,4,2,32,256]{4,3,2,1,0:T(8,128)(2,1)}, bf16[3,4,2,32,256]{4,3,2,1,0:T(8,128)(2,1)}, f32[2,4,256]{2,1,0:T(4,128)}) custom-call(bf16[6,4,2,32,256]{4,3,2,1,0:T(8,128)(2,1)} %get-tuple-element.6.landed, bf16[2,3,2,32,256]{4,3,2,1,0:T(8,128)(2,1)} %get-tuple-element.7.halo, f32[2,4,256]{2,1,0:T(4,128)} %get-tuple-element.8.energy), custom_call_target="tpu_custom_call" | custom-call | tf_op jit(solution)/shard_map/closing/pallas_call | solution.py:970

commit v5 on v4

--- a/solution.py
+++ b/solution.py
@@ -882,13 +882,17 @@
     induced = [copy(landed.at[pl.ds(3, 3), s], ind.at[:, s], isem.at[3 + s]) for s in range(shells)]
     advected = copy(landed.at[pl.ds(0, 3)], adv, isem.at[1])
     energies = copy(energy, total, isem.at[2])
+    advected.start()
+    energies.start()
     halos.start()
     for shell in induced:
         shell.start()
-    advected.start()
-    energies.start()
     outs = [copy(grad.at[:, s], grad_out.at[:, s], osem.at[2 + s]) for s in range(shells)]
     outs += [copy(adv, adv_out, osem.at[0]), copy(total, energy_out, osem.at[1])]
+    advected.wait()
+    outs[shells].start()
+    energies.wait()
+    outs[shells + 1].start()
     halos.wait()
     induced[0].wait()
     for s in range(shells):
@@ -900,10 +904,6 @@
         before = ind[:, s - 1].astype(F32) if s > 0 else jnp.where(rad > 0, rim[0].astype(F32), 0.0)
         grad[:, s] = ((after - before) * 0.5).astype(BF)
         outs[s].start()
-    advected.wait()
-    outs[shells].start()
-    energies.wait()
-    outs[shells + 1].start()
     for out in outs:
         out.wait()
 

time: 58.7 us -> 58.6 us (level)
  no operation moved by 1% of the time
where the time goes in v5:
time: 58.6 us; the launch traced here: 58.3 us
  Pallas kernels  57.5 us (98%)
  between operations  0.8 us (1%)
    pallas_call x1, Pallas kernels, local_relay(): pl.pallas_call(functools.partial(relay_kernel, dims), name='dynamo', out_...  55.4 us
    pallas_call x1, Pallas kernels, local_relay(): pl.pallas_call(functools.partial(closing_kernel, rads, shells), name='clo...  2.07 us

profile of v5, /device:TPU:8, one launch (start us, length us, event | category | flops | bytes accessed | tf_op | source)
XLA Modules:
  0.0 58.3 jit_solution(875974134609499069)
XLA Ops:
  0.6 55.4 %dynamo.1 = (bf16[6,4,2,32,256]{4,3,2,1,0:T(8,128)(2,1)}, bf16[2,3,2,32,256]{4,3,2,1,0:T(8,128)(2,1)}, f32[2,4,256]{2,1,0:T(4,128)}) custom-call(bf16[3,4,2,32,256]{4,3,2,1,0:T(8,128)(2,1)} %vel_ref.1, bf16[3,4,2,32,256]{4,3,2,1,0:T(8,128)(2,1)} %mag_ref.1, bf16[3,4,2,32,256]{4,3,2,1,0:T(8,128)(2,1)} %vor_ref.1, bf16[3,4,2,32,256]{4,3,2,1,0:T(8,128)(2,1)} %cur_ref.1, ...), custom_call_target="tpu_custom_call" | custom-call | tf_op jit(solution)/shard_map/dynamo/pallas_call | solution.py:923
  56.1 2.1 %closing.1 = (bf16[3,4,2,32,256]{4,3,2,1,0:T(8,128)(2,1)}, bf16[3,4,2,32,256]{4,3,2,1,0:T(8,128)(2,1)}, f32[2,4,256]{2,1,0:T(4,128)}) custom-call(bf16[6,4,2,32,256]{4,3,2,1,0:T(8,128)(2,1)} %get-tuple-element.6.landed, bf16[2,3,2,32,256]{4,3,2,1,0:T(8,128)(2,1)} %get-tuple-element.7.halo, f32[2,4,256]{2,1,0:T(4,128)} %get-tuple-element.8.energy), custom_call_target="tpu_custom_call" | custom-call | tf_op jit(solution)/shard_map/closing/pallas_call | solution.py:970
